TPU v7x, 32 devices: a whole 2x2x4 slice. The times are simulated.
32 devices in a mesh: blk: 16 (over z, y, x), obs: 2 (over core).
Axes of the slice: x: 2, y: 2, z: 4, core: 2. Of those that a mesh axis runs over, the one named last changes fastest.
Arguments:
- populations: float32 [16, 19, 32, 1024], P('blk', None, 'obs'), may hold values from 0.011111111 to 0.533333333, as said below
- block_faces: int32 [16, 4], P('blk'), may hold values from 0 to 15, as said below
- block_edges: int32 [16, 4], P('blk'), may hold values from 0 to 15, as said below
- probe_cell: int32 [4096], P(('blk', 'obs')), may hold values from 0 to 16383
- history: bfloat16 [4096, 512], P(('blk', 'obs')), may hold values from -6 to 6
- panel_count: int32 [32], P(('blk', 'obs')), may hold values from 0 to 128, as said below
- panel_owner: int32 [4096], P(('blk', 'obs')), may hold values from 0 to 1023, as said below
- panel_pos: bfloat16 [3, 2048], P(None, ('blk', 'obs')), may hold values from -1 to 1
- panel_normal: bfloat16 [3, 2048], P(None, ('blk', 'obs')), may hold values from -0.625 to 0.625
- observers: float32 [3, 1024], P(None, 'obs'), may hold values from -8 to 8, as said below
Outputs:
- populations_out: float32 [16, 19, 32, 1024], P('blk', None, 'obs')
- spectrum: float32 [2, 512, 128], P('obs', 'blk')
Inputs may be any that keep to these rules, and one draw needn't show every extreme that they name: `populations`: every population is positive. The blocks form a lattice of 4 by 4 blocks along y and z, periodic in both, one block deep in x; block_faces[b] names the blocks beside b at -y, +y, -z, +z. block_edges[b] names the blocks at (-y,-z), (-y,+z), (+y,-z), (+y,+z) of b: the y neighbour's z neighbour, which is the z neighbour's y neighbour. The eight face and edge neighbours of a block are distinct and differ from it. The live slots of a device are its first panel_count slots. The counts of the devices at one obs index sum to 1024. `panel_owner`: in a live slot of the device at blk index b and obs index o the value is q * 64 + j: slot j of the owner at blk index q and the same obs index. Every owner slot receives exactly one live panel. A device sends at most 8 live panels to one owner, and its live panels go to the owners in numbers that differ by at most one. Dead slots hold arbitrary values of the range. `observers`: every observer lies at a distance of 4 to 8 from the anchor (0, 0, 0).
All inputs are finite; a program needn't handle non-finite values.
Results may differ from a plain program's by a relative error of at most 0.0032.
The roundings to bfloat16 on the way count: a program that leaves them out, or rounds other values in their place, can miss the bound.
Values may be sent and summed in bfloat16 or wider, within the bound.
A program may use at most 128 MiB of HBM per device.

v0:
```python
import math

import jax
import jax.numpy as jnp
from jax import lax
from jax.sharding import PartitionSpec as P

BS = 32
STEPS = 4
SAMPLES = 256
BINS = 64
P_OWN = 64


velocity_list = [
    (0, 0, 0),
    (1, 0, 0),
    (-1, 0, 0),
    (0, 1, 0),
    (0, -1, 0),
    (0, 0, 1),
    (0, 0, -1),
    (1, 1, 0),
    (-1, -1, 0),
    (1, -1, 0),
    (-1, 1, 0),
    (1, 0, 1),
    (-1, 0, -1),
    (1, 0, -1),
    (-1, 0, 1),
    (0, 1, 1),
    (0, -1, -1),
    (0, 1, -1),
    (0, -1, 1),
]
weight_list = [1.0 / 3.0] + [1.0 / 18.0] * 6 + [1.0 / 36.0] * 12
x_moving = [1, 2, 7, 8, 9, 10, 11, 12, 13, 14]
y_upward = [3, 7, 10, 15, 17]
y_downward = [4, 8, 9, 16, 18]
z_upward = [5, 11, 14, 15, 18]
z_downward = [6, 12, 13, 16, 17]
relax_rate = 1.6
pressure_gain = 60.0
sound_speed = 0.5


def padded(block, sides, width):
    for axis, dim in sides:
        count = lax.axis_size(axis)
        forward = [(i, i + 1) for i in range(count - 1)]
        forward.append((count - 1, 0))
        backward = [(target, source) for source, target in forward]
        low = lax.ppermute(
            lax.slice_in_dim(block, block.shape[dim] - width, None, axis=dim), axis, forward
        )
        high = lax.ppermute(lax.slice_in_dim(block, 0, width, axis=dim), axis, backward)
        block = jnp.concatenate([low, block, high], axis=dim)
    return block


def component(axis_number, extra):
    values = jnp.array([velocity[axis_number] for velocity in velocity_list], jnp.float32)
    return values.reshape((19,) + extra)


def collide(field):
    extra = (1,) * (field.ndim - 1)
    along_x = component(0, extra)
    along_y = component(1, extra)
    along_z = component(2, extra)
    weights = jnp.array(weight_list, jnp.float32).reshape((19,) + extra)
    density = jnp.sum(field, axis=0)
    speed_x = jnp.sum(along_x * field, axis=0) / density
    speed_y = jnp.sum(along_y * field, axis=0) / density
    speed_z = jnp.sum(along_z * field, axis=0) / density
    projected = along_x * speed_x + along_y * speed_y + along_z * speed_z
    squared = speed_x * speed_x + speed_y * speed_y + speed_z * speed_z
    equilibrium = (
        weights * density * (1.0 + 3.0 * projected + 4.5 * projected * projected - 1.5 * squared)
    )
    return field + relax_rate * (equilibrium - field)


def stream_merged(widened, planes):
    below_plane, above_plane, near_plane, far_plane = planes
    slab_depth = widened.shape[1] - 2
    lane_count = widened.shape[2]
    lane_index = jnp.arange(lane_count, dtype=jnp.int32)
    lane_row = lane_index // BS
    lane_column = lane_index % BS
    parts = []
    for number, velocity in enumerate(velocity_list):
        shift_x, shift_y, shift_z = velocity
        begin = 1 - shift_x
        moved = jnp.roll(
            widened[number, begin : begin + slab_depth], shift_y * BS + shift_z, axis=-1
        )
        if shift_y != 0:
            source_plane = below_plane if shift_y == 1 else above_plane
            row_values = jnp.roll(
                source_plane[number, begin : begin + slab_depth], shift_z, axis=-1
            )
            edge_index = 0 if shift_y == 1 else BS - 1
            moved = jnp.where(
                (lane_row == edge_index)[None, :], jnp.tile(row_values, (1, BS)), moved
            )
        if shift_z != 0:
            source_plane = near_plane if shift_z == 1 else far_plane
            column_values = source_plane[
                number, begin : begin + slab_depth, 1 - shift_y : 1 - shift_y + BS
            ]
            edge_index = 0 if shift_z == 1 else BS - 1
            moved = jnp.where(
                (lane_column == edge_index)[None, :], jnp.repeat(column_values, BS, axis=-1), moved
            )
        parts.append(moved)
    return jnp.stack(parts)


def place_pieces(pieces, targets, blocks):
    onehot = (targets[:, None] == jnp.arange(blocks, dtype=jnp.int32)[None, :]).astype(jnp.float32)
    return jnp.einsum("kn,kf->nf", onehot, pieces, precision=lax.Precision.HIGHEST)


def spread_pops(piece, chosen, shape):
    return jnp.zeros(shape, jnp.float32).at[jnp.array(chosen)].set(piece)


def direct_halo(widened, block_faces, block_edges, blocks):
    depth_x = widened.shape[1]
    lane_count = widened.shape[2]

    def corner_piece(number, lane_at):
        return jnp.zeros((5, depth_x, BS), jnp.float32).at[0, :, 0].set(widened[number, :, lane_at])

    def corner_plane(number, vector):
        return jnp.zeros((19, depth_x, 1), jnp.float32).at[number, :, 0].set(vector)

    outgoing = jnp.stack(
        [
            widened[jnp.array(y_downward), :, 0:BS],
            widened[jnp.array(y_upward), :, lane_count - BS :],
            widened[jnp.array(z_downward), :, 0::BS],
            widened[jnp.array(z_upward), :, BS - 1 :: BS],
            corner_piece(16, 0),
            corner_piece(18, BS - 1),
            corner_piece(17, (BS - 1) * BS),
            corner_piece(15, BS * BS - 1),
        ]
    ).reshape(8, -1)
    targets = jnp.concatenate([block_faces, block_edges])
    received = lax.all_to_all(
        place_pieces(outgoing, targets, blocks), "blk", split_axis=0, concat_axis=0, tiled=True
    )
    chosen = jnp.take(received, targets, axis=0).reshape(8, 5, depth_x, BS)
    below_plane = spread_pops(chosen[0], y_upward, (19, depth_x, BS))
    above_plane = spread_pops(chosen[1], y_downward, (19, depth_x, BS))
    near_core = spread_pops(chosen[2], z_upward, (19, depth_x, BS))
    far_core = spread_pops(chosen[3], z_downward, (19, depth_x, BS))
    near_plane = jnp.concatenate(
        [corner_plane(15, chosen[4, 0, :, 0]), near_core, corner_plane(18, chosen[6, 0, :, 0])],
        axis=2,
    )
    far_plane = jnp.concatenate(
        [corner_plane(17, chosen[5, 0, :, 0]), far_core, corner_plane(16, chosen[7, 0, :, 0])],
        axis=2,
    )
    return (below_plane, above_plane, near_plane, far_plane)


def transform_table():
    moments = jnp.arange(SAMPLES, dtype=jnp.int32)[:, None]
    harmonics = jnp.arange(BINS, dtype=jnp.int32)[None, :] + 1
    turns = moments * harmonics % SAMPLES
    phases = turns.astype(jnp.float32) * (2.0 * math.pi / SAMPLES)
    return jnp.concatenate([jnp.cos(phases), -jnp.sin(phases)], axis=1).astype(jnp.bfloat16)


def radiate(spectra, place, normal, listen):
    values = spectra.astype(jnp.float32)
    press_real = values[0:BINS].T
    press_imag = values[BINS : 2 * BINS].T
    rate_real = values[2 * BINS : 3 * BINS].T
    rate_imag = values[3 * BINS : 4 * BINS].T
    offsets = listen[:, None, :] - place.astype(jnp.float32)[:, :, None]
    distance_sq = jnp.sum(offsets * offsets, axis=0)
    distance = jnp.sqrt(distance_sq)
    facing = jnp.sum(normal.astype(jnp.float32)[:, :, None] * offsets, axis=0)
    far_term = facing / (4.0 * math.pi * sound_speed * distance_sq)
    near_term = facing / (4.0 * math.pi * distance_sq * distance)
    angular = (jnp.arange(BINS, dtype=jnp.float32) + 1.0) * (2.0 * math.pi / SAMPLES)
    phases = angular[None, :, None] * (distance / sound_speed)[:, None, :]
    cosine = jnp.cos(phases)
    sine_part = jnp.sin(phases)
    weight_real = (
        far_term[:, None, :] * rate_real[:, :, None]
        + near_term[:, None, :] * press_real[:, :, None]
    )
    weight_imag = (
        far_term[:, None, :] * rate_imag[:, :, None]
        + near_term[:, None, :] * press_imag[:, :, None]
    )
    real_part = jnp.sum(weight_real * cosine + weight_imag * sine_part, axis=0)
    imag_part = jnp.sum(weight_imag * cosine - weight_real * sine_part, axis=0)
    return jnp.concatenate([real_part, imag_part], axis=0).T


def radiate_blocks(spectra, place, normal, listen):
    count_panels = spectra.shape[1]
    listener_count = listen.shape[1]
    block_size = 128
    while block_size > 1 and (
        count_panels % block_size != 0 or block_size * listener_count > 16384
    ):
        block_size = block_size // 2

    def radiate_accumulate(block_number, total):
        begin = block_number * block_size
        return total + radiate(
            lax.dynamic_slice_in_dim(spectra, begin, block_size, 1),
            lax.dynamic_slice_in_dim(place, begin, block_size, 1),
            lax.dynamic_slice_in_dim(normal, begin, block_size, 1),
            listen,
        )

    return lax.fori_loop(
        0,
        count_panels // block_size,
        radiate_accumulate,
        jnp.zeros((listener_count, 2 * BINS), jnp.float32),
    )


def route_slots(payload, owners, alive_slot, blocks):
    count_slots = payload.shape[0]
    capacity = -(-count_slots // blocks)
    target = owners // P_OWN
    member = (
        (target[:, None] == jnp.arange(blocks, dtype=jnp.int32)[None, :]) & alive_slot[:, None]
    ).astype(jnp.int32)
    before = jnp.cumsum(member, axis=0) - member
    order_within = jnp.sum(before * member, axis=1)
    slot_label = jnp.where(alive_slot, target * capacity + order_within, -1)
    matches = slot_label[:, None] == jnp.arange(blocks * capacity, dtype=jnp.int32)[None, :]
    source = jnp.sum(
        jnp.where(matches, jnp.arange(count_slots, dtype=jnp.int32)[:, None], 0), axis=0
    )
    filled = jnp.any(matches, axis=0)
    outgoing = jnp.take(payload, source, axis=0).reshape(blocks, capacity, payload.shape[1])
    tagged = jnp.where(filled, jnp.take(owners, source), -1).reshape(blocks, capacity)
    return (outgoing, tagged)


def settle(incoming, tagged):
    keeper = lax.axis_index("blk")
    flat_tags = tagged.reshape(-1)
    slot_here = flat_tags - keeper * P_OWN
    choose = (
        (slot_here[:, None] == jnp.arange(P_OWN, dtype=jnp.int32)[None, :])
        & (flat_tags[:, None] >= 0)
    ).astype(jnp.bfloat16)
    return jnp.einsum(
        "rw,rp->wp",
        incoming.reshape(-1, incoming.shape[-1]),
        choose,
        preferred_element_type=jnp.float32,
    ).astype(jnp.bfloat16)


def body(
    populations,
    block_faces,
    block_edges,
    probe_cell,
    history,
    panel_count,
    panel_owner,
    panel_pos,
    panel_normal,
    observers,
):
    blocks = lax.axis_size("blk")
    lattice_state = populations[0]
    slab_depth = lattice_state.shape[1]
    lane_count = lattice_state.shape[2]
    faces_here = block_faces[0]
    edges_here = block_edges[0]
    readings = []
    for turn_index in range(STEPS):
        collided = collide(lattice_state)
        slab_edges = padded(collided[jnp.array(x_moving)], (("obs", 1),), 1)
        lower_plane = spread_pops(slab_edges[:, 0:1], x_moving, (19, 1, lane_count))
        upper_plane = spread_pops(slab_edges[:, -1:], x_moving, (19, 1, lane_count))
        widened = jnp.concatenate([lower_plane, collided, upper_plane], axis=1)
        planes = direct_halo(widened, faces_here, edges_here, blocks)
        lattice_state = stream_merged(widened, planes)
        density = jnp.sum(lattice_state, axis=0).reshape(-1)
        readings.append(jnp.take(density, probe_cell))
    populations_out = lattice_state.reshape(1, 19, slab_depth, lane_count)
    gained = pressure_gain * (jnp.stack(readings, axis=1) - 1.0)
    previous = jnp.concatenate(
        [history[:, SAMPLES - 1 : SAMPLES].astype(jnp.float32), gained[:, :-1]], axis=1
    )
    rate_values = gained - previous
    recent = jnp.concatenate(
        [
            history[:, STEPS:SAMPLES],
            gained.astype(jnp.bfloat16),
            history[:, SAMPLES + STEPS :],
            rate_values.astype(jnp.bfloat16),
        ],
        axis=1,
    )
    transform = transform_table()
    count_slots = recent.shape[0]
    alive_slot = jnp.arange(count_slots, dtype=jnp.int32) < panel_count[0]
    outgoing, tagged = route_slots(recent, panel_owner, alive_slot, blocks)
    incoming, tags_in = (
        lax.all_to_all(outgoing, "blk", split_axis=0, concat_axis=0, tiled=True),
        lax.all_to_all(tagged, "blk", split_axis=0, concat_axis=0, tiled=True),
    )
    histories = settle(incoming, tags_in).reshape(2, SAMPLES, P_OWN)
    spectra = (
        jnp.einsum("tk,gtp->gkp", transform, histories, preferred_element_type=jnp.float32)
        .astype(jnp.bfloat16)
        .reshape(4 * BINS, P_OWN)
    )
    partial_value = radiate_blocks(
        lax.all_gather(spectra, "obs", axis=1, tiled=True),
        lax.all_gather(panel_pos, "obs", axis=1, tiled=True),
        lax.all_gather(panel_normal, "obs", axis=1, tiled=True),
        observers,
    )
    summed = lax.psum_scatter(partial_value, "blk", scatter_dimension=0, tiled=True)
    return (populations_out, summed.reshape(1, -1, 2 * BINS))


def solution(mesh):
    placed = (
        P("blk", None, "obs", None),
        P("blk", None),
        P("blk", None),
        P(("blk", "obs")),
        P(("blk", "obs"), None),
        P(("blk", "obs")),
        P(("blk", "obs")),
        P(None, ("blk", "obs")),
        P(None, ("blk", "obs")),
        P(None, "obs"),
    )
    return jax.shard_map(
        body,
        mesh=mesh,
        in_specs=placed,
        out_specs=(P("blk", None, "obs", None), P("obs", "blk", None)),
        check_vma=False,
    )
```

profile of v0, /device:TPU:0, one launch (start us, length us, event | category | flops | bytes accessed | tf_op | source)
XLA Modules:
  0.0 674.4 jit_solution(10351201009113472713)
XLA Ops:
  8.0 1.4 reduce_sum.891
  10.0 1.3 fusion.16
  16.9 1.2 gather_fusion.21
  21.0 1.9 all-gather.1
  23.0 1.8 all-gather
  56.1 5.3 copy.672
  61.4 7.4 %copy.668 = f32[19,18,1024]{1,0,2:T(8,128)} copy(f32[19,18,1024]{2,1,0:T(8,128)S(1)} %pad_maximum_fusion) | data formatting | bytes 2801664 | tf_op jit(solution)/shard_map/concatenate | solution.py:294
  69.6 2.6 gather_fusion.4
  72.2 2.6 gather_fusion.3
  75.3 1.5 gather_fusion.2
  76.9 1.5 gather_fusion.1
  80.4 8.7 %all-to-all-start = ((f32[16,1,2880]{2,1,0:T(1,128)}), f32[16,1,2880]{2,1,0:T(1,128)S(1)}, u32[]{:S(2)}, u32[]{:S(2)}) async-start(f32[16,1,2880]{2,1,0:T(1,128)} %copy.680), calls=%async_computation | async-start | bytes 376832 | tf_op jit(solution)/shard_map/all_to_all | solution.py:152
  138.3 1.0 constant_dynamic-update-slice_fusion.15
  141.3 1.0 constant_dynamic-update-slice_fusion.12
  151.7 1.3 fusion.22
  155.6 1.6 select_add_fusion.3
  157.1 1.3 gather_fusion.26
  159.8 1.3 scatter_custom_fusion.6
  184.5 5.2 copy.695
  189.7 3.3 gather_fusion.9
  193.0 3.3 gather_fusion.8
  196.3 7.4 %copy.691 = f32[19,18,1024]{1,0,2:T(8,128)} copy(f32[19,18,1024]{2,1,0:T(8,128)S(1)} %pad_maximum_fusion.1) | data formatting | bytes 2801664 | tf_op jit(solution)/shard_map/concatenate | solution.py:294
  203.7 1.5 gather_fusion.7
  205.2 1.5 gather_fusion.6
  210.0 7.4 %all-to-all-start.1 = ((f32[16,1,2880]{2,1,0:T(1,128)}), f32[16,1,2880]{2,1,0:T(1,128)S(1)}, u32[]{:S(2)}, u32[]{:S(2)}) async-start(f32[16,1,2880]{2,1,0:T(1,128)} %copy.703), calls=%async_computation.1 | async-start | bytes 376832 | tf_op jit(solution)/shard_map/all_to_all | solution.py:152
  269.7 1.0 constant_dynamic-update-slice_fusion.31
  280.1 1.3 fusion.28
  284.0 1.6 select_add_fusion.2
  285.5 1.8 gather_fusion.27
  288.2 1.0 scatter_custom_fusion.12
  312.6 5.2 copy.718
  317.8 3.3 gather_fusion.14
  321.1 3.3 gather_fusion.13
  324.4 7.4 %copy.714 = f32[19,18,1024]{1,0,2:T(8,128)} copy(f32[19,18,1024]{2,1,0:T(8,128)S(1)} %pad_maximum_fusion.2) | data formatting | bytes 2801664 | tf_op jit(solution)/shard_map/concatenate | solution.py:294
  331.8 1.5 gather_fusion.12
  333.3 1.5 gather_fusion.11
  338.1 7.6 %all-to-all-start.2 = ((f32[16,1,2880]{2,1,0:T(1,128)}), f32[16,1,2880]{2,1,0:T(1,128)S(1)}, u32[]{:S(2)}, u32[]{:S(2)}) async-start(f32[16,1,2880]{2,1,0:T(1,128)} %copy.726), calls=%async_computation.2 | async-start | bytes 376832 | tf_op jit(solution)/shard_map/all_to_all | solution.py:152
  398.0 1.0 constant_dynamic-update-slice_fusion.50
  408.4 1.3 fusion.34
  412.3 1.6 select_add_fusion.1
  413.8 1.9 gather_fusion.28
  430.3 5.2 copy.741
  435.5 2.6 gather_fusion.19
  438.1 2.6 gather_fusion.18
  440.8 7.4 %copy.737 = f32[19,18,1024]{1,0,2:T(8,128)} copy(f32[19,18,1024]{2,1,0:T(8,128)S(1)} %pad_maximum_fusion.3) | data formatting | bytes 2801664 | tf_op jit(solution)/shard_map/concatenate | solution.py:294
  448.2 1.5 gather_fusion.17
  449.7 1.5 gather_fusion.16
  454.3 7.2 %all-to-all-start.3 = ((f32[16,1,2880]{2,1,0:T(1,128)}), f32[16,1,2880]{2,1,0:T(1,128)S(1)}, u32[]{:S(2)}, u32[]{:S(2)}) async-start(f32[16,1,2880]{2,1,0:T(1,128)} %copy.749), calls=%async_computation.3 | async-start | bytes 376832 | tf_op jit(solution)/shard_map/all_to_all | solution.py:152
  464.2 5.7 all-to-all-done.3
  469.9 3.8 all-to-all-start.5
  485.9 1.6 fusion.114
  487.5 1.6 fusion.113
  489.9 1.6 fusion.111
  491.5 1.6 fusion.110
  501.9 1.3 gather_fusion.29
  505.4 7.0 %all-to-all-start.4 = ((bf16[16,8,512]{2,1,0:T(8,128)(2,1)}), bf16[16,8,512]{2,1,0:T(8,128)(2,1)S(1)}, u32[]{:S(2)}, u32[]{:S(2)}) async-start(bf16[16,8,512]{2,1,0:T(8,128)(2,1)} %bitcast_select_fusion), calls=%async_computation.4 | async-start | bytes 262144 | tf_op jit(solution)/shard_map/all_to_all | solution.py:319
  512.7 7.5 %all-to-all-done.4 = bf16[16,8,512]{2,1,0:T(8,128)(2,1)S(1)} async-done(((bf16[16,8,512]{2,1,0:T(8,128)(2,1)}), bf16[16,8,512]{2,1,0:T(8,128)(2,1)S(1)}, u32[]{:S(2)}, u32[]{:S(2)}) %all-to-all-start.4) | async-done | bytes 131104 | tf_op jit(solution)/shard_map/all_to_all | solution.py:319
  520.7 2.1 all_gather.11
  522.8 69.2 %while.46 = (s32[]{:T(128)}, f32[512,128]{0,1:T(8,128)S(1)}, bf16[3,128]{1,0:T(4,128)(2,1)S(1)}, f32[3,512]{1,0:T(4,128)S(1)}, bf16[3,128]{1,0:T(4,128)(2,1)S(1)...) while((s32[]{:T(128)}, f32[512,128]{0,1:T(8,128)S(1)}, ...), condition=%wide.region_46.49_spmd.clone, body=%wide.region_41.48_spmd.clone.sunk | while | flops 16179527 | bytes 1860141 | solution.py:226
  523.1 16.8 %fusion.295 = (f32[64,512]{1,0:T(8,128)S(1)}, f32[64,512]{1,0:T(8,128)S(1)}) fusion(f32[32,64]{1,0:T(8,128)S(1)} %get-tuple-element.1175, f32[32,64]{1,0:T(8,128)S(1)} %get-tuple-element.1176, f32[32,512]{1,0:T(8,128)S(1)} %get-tuple-element.1181, f32[64]{0:T(128)S(1)} %add_multiply_fusion.3, f32[32,64]{1,0:T(8,128)S(1)} %get-tuple-element.1182, ...), kind=kLoop, calls=%fused_computation.61.clone.1 | loop fusion | flops 15663104 | bytes 491776 | tf_op jit(solution)/shard_map/while/body/eval_jaxpr/reduce_sum | solution.py:203
  540.4 16.8 %fusion.295 = (f32[64,512]{1,0:T(8,128)S(1)}, f32[64,512]{1,0:T(8,128)S(1)}) fusion(f32[32,64]{1,0:T(8,128)S(1)} %get-tuple-element.1175, f32[32,64]{1,0:T(8,128)S(1)} %get-tuple-element.1176, f32[32,512]{1,0:T(8,128)S(1)} %get-tuple-element.1181, f32[64]{0:T(128)S(1)} %add_multiply_fusion.3, f32[32,64]{1,0:T(8,128)S(1)} %get-tuple-element.1182, ...), kind=kLoop, calls=%fused_computation.61.clone.1 | loop fusion | flops 15663104 | bytes 491776 | tf_op jit(solution)/shard_map/while/body/eval_jaxpr/reduce_sum | solution.py:203
  557.7 16.8 %fusion.295 = (f32[64,512]{1,0:T(8,128)S(1)}, f32[64,512]{1,0:T(8,128)S(1)}) fusion(f32[32,64]{1,0:T(8,128)S(1)} %get-tuple-element.1175, f32[32,64]{1,0:T(8,128)S(1)} %get-tuple-element.1176, f32[32,512]{1,0:T(8,128)S(1)} %get-tuple-element.1181, f32[64]{0:T(128)S(1)} %add_multiply_fusion.3, f32[32,64]{1,0:T(8,128)S(1)} %get-tuple-element.1182, ...), kind=kLoop, calls=%fused_computation.61.clone.1 | loop fusion | flops 15663104 | bytes 491776 | tf_op jit(solution)/shard_map/while/body/eval_jaxpr/reduce_sum | solution.py:203
  575.0 16.8 %fusion.295 = (f32[64,512]{1,0:T(8,128)S(1)}, f32[64,512]{1,0:T(8,128)S(1)}) fusion(f32[32,64]{1,0:T(8,128)S(1)} %get-tuple-element.1175, f32[32,64]{1,0:T(8,128)S(1)} %get-tuple-element.1176, f32[32,512]{1,0:T(8,128)S(1)} %get-tuple-element.1181, f32[64]{0:T(128)S(1)} %add_multiply_fusion.3, f32[32,64]{1,0:T(8,128)S(1)} %get-tuple-element.1182, ...), kind=kLoop, calls=%fused_computation.61.clone.1 | loop fusion | flops 15663104 | bytes 491776 | tf_op jit(solution)/shard_map/while/body/eval_jaxpr/reduce_sum | solution.py:203
  592.8 74.4 %reduce-scatter.2.cloned.1.call-done = f32[32,128]{1,0:T(8,128)} async-done(((f32[512,128]{1,0:T(8,128)}), f32[32,128]{1,0:T(8,128)}) %reduce-scatter.2.cloned.1.call-update) | async-done | bytes 16400 | tf_op jit(solution)/shard_map/reduce_scatter | solution.py:334
  (1784 shorter events, 331.1 us)
Async XLA Ops:
  11.5 11.5 %copy-start.426 = (bf16[3,64]{1,0:T(4,128)(2,1)S(1)}, bf16[3,64]{1,0:T(4,128)(2,1)}, u32[]{:S(2)}) copy-start(bf16[3,64]{1,0:T(4,128)(2,1)} %param.148) | copy-start | bytes 1156
  12.2 19.8 %collective-permute-start = (f32[10,1,1024]{2,1,0:T(1,128)S(1)}, f32[10,1,1024]{2,1,0:T(1,128)S(1)}, u32[]{:S(2)}, u32[]{:S(2)}) collective-permute-start(f32[10,1,1024]{2,1,0:T(1,128)S(1)} %get-tuple-element.752), channel_id=1, source_target_pairs={{0,1},{1,0},{2,3},{3,2},{4,5},{5,4},{6,7},{7,6},{8,9},{9,8},{10,11... | collective-permute-start | bytes 122888 | tf_op jit(solution)/shard_map/ppermute | solution.py:53
  12.7 18.4 %collective-permute-start.1 = (f32[10,1,1024]{2,1,0:T(1,128)S(1)}, f32[10,1,1024]{2,1,0:T(1,128)S(1)}, u32[]{:S(2)}, u32[]{:S(2)}) collective-permute-start(f32[10,1,1024]{2,1,0:T(1,128)S(1)} %get-tuple-element.753), channel_id=1, source_target_pairs={{1,0},{0,1},{3,2},{2,3},{5,4},{4,5},{7,6},{6,7},{9,8},{8,9},{11,10... | collective-permute-start | bytes 122888 | tf_op jit(solution)/shard_map/ppermute | solution.py:56
  16.8 14.2 %copy-start.420 = (s32[1024]{0:T(1024)}, s32[1024]{0:T(1024)S(1)}, u32[]{:S(2)}) copy-start(s32[1024]{0:T(1024)S(1)} %get-tuple-element.1095) | copy-start | bytes 12292
  76.8 12.3 %copy-start.161 = (f32[16,992]{1,0:T(8,128)S(1)}, f32[16,992]{1,0:T(8,128)}, u32[]{:S(2)}) copy-start(f32[16,992]{1,0:T(8,128)} %get-tuple-element.1039) | copy-start | bytes 190468
  76.8 12.3 %copy-start.320 = (f32[16,32]{1,0:T(8,128)S(1)}, f32[16,32]{1,0:T(8,128)}, u32[]{:S(2)}) copy-start(f32[16,32]{1,0:T(8,128)} %get-tuple-element.1037) | copy-start | bytes 6148
  76.8 12.4 %copy-start.164 = (f32[16,992]{1,0:T(8,128)S(1)}, f32[16,992]{1,0:T(8,128)}, u32[]{:S(2)}) copy-start(f32[16,992]{1,0:T(8,128)} %get-tuple-element.1045) | copy-start | bytes 190468
  76.8 12.4 %copy-start.323 = (f32[16,32]{1,0:T(8,128)S(1)}, f32[16,32]{1,0:T(8,128)}, u32[]{:S(2)}) copy-start(f32[16,32]{1,0:T(8,128)} %get-tuple-element.1047) | copy-start | bytes 6148
  76.8 12.5 %copy-start.167 = (f32[16,1023]{1,0:T(8,128)S(1)}, f32[16,1023]{1,0:T(8,128)}, u32[]{:S(2)}) copy-start(f32[16,1023]{1,0:T(8,128)} %get-tuple-element.1055) | copy-start | bytes 196420
  76.9 12.5 %copy-start.326 = (f32[16,1]{1,0:T(8,128)S(1)}, f32[16,1]{1,0:T(8,128)}, u32[]{:S(2)}) copy-start(f32[16,1]{1,0:T(8,128)} %get-tuple-element.1053) | copy-start | bytes 196
  76.9 12.5 %copy-start.170 = (f32[16,992]{1,0:T(8,128)S(1)}, f32[16,992]{1,0:T(8,128)}, u32[]{:S(2)}) copy-start(f32[16,992]{1,0:T(8,128)} %get-tuple-element.1041) | copy-start | bytes 190468
  76.9 12.5 %copy-start.329 = (f32[16,32]{1,0:T(8,128)S(1)}, f32[16,32]{1,0:T(8,128)}, u32[]{:S(2)}) copy-start(f32[16,32]{1,0:T(8,128)} %get-tuple-element.1043) | copy-start | bytes 6148
  78.4 11.1 %copy-start.173 = (f32[16,992]{1,0:T(8,128)S(1)}, f32[16,992]{1,0:T(8,128)}, u32[]{:S(2)}) copy-start(f32[16,992]{1,0:T(8,128)} %get-tuple-element.1051) | copy-start | bytes 190468
  78.4 11.1 %copy-start.332 = (f32[16,32]{1,0:T(8,128)S(1)}, f32[16,32]{1,0:T(8,128)}, u32[]{:S(2)}) copy-start(f32[16,32]{1,0:T(8,128)} %get-tuple-element.1049) | copy-start | bytes 6148
  78.4 11.2 %copy-start.176 = (f32[16,1023]{1,0:T(8,128)S(1)}, f32[16,1023]{1,0:T(8,128)}, u32[]{:S(2)}) copy-start(f32[16,1023]{1,0:T(8,128)} %get-tuple-element.1057) | copy-start | bytes 196420
  78.4 11.2 %copy-start.335 = (f32[16,1]{1,0:T(8,128)S(1)}, f32[16,1]{1,0:T(8,128)}, u32[]{:S(2)}) copy-start(f32[16,1]{1,0:T(8,128)} %get-tuple-element.1059) | copy-start | bytes 196
  78.6 11.1 %copy-start.179 = (f32[16,1023]{1,0:T(8,128)S(1)}, f32[16,1023]{1,0:T(8,128)}, u32[]{:S(2)}) copy-start(f32[16,1023]{1,0:T(8,128)} %get-tuple-element.1067) | copy-start | bytes 196420
  78.6 11.1 %copy-start.338 = (f32[16,1]{1,0:T(8,128)S(1)}, f32[16,1]{1,0:T(8,128)}, u32[]{:S(2)}) copy-start(f32[16,1]{1,0:T(8,128)} %get-tuple-element.1065) | copy-start | bytes 196
  78.6 11.2 %copy-start.184 = (f32[16,1023]{1,0:T(8,128)S(1)}, f32[16,1023]{1,0:T(8,128)}, u32[]{:S(2)}) copy-start(f32[16,1023]{1,0:T(8,128)} %get-tuple-element.1061) | copy-start | bytes 196420
  78.6 11.2 %copy-start.341 = (f32[16,1]{1,0:T(8,128)S(1)}, f32[16,1]{1,0:T(8,128)}, u32[]{:S(2)}) copy-start(f32[16,1]{1,0:T(8,128)} %get-tuple-element.1063) | copy-start | bytes 196
  78.7 11.2 %copy-start.191 = (f32[16,992]{1,0:T(8,128)S(1)}, f32[16,992]{1,0:T(8,128)}, u32[]{:S(2)}) copy-start(f32[16,992]{1,0:T(8,128)} %get-tuple-element.1023) | copy-start | bytes 190468
  78.7 11.2 %copy-start.347 = (f32[16,32]{1,0:T(8,128)S(1)}, f32[16,32]{1,0:T(8,128)}, u32[]{:S(2)}) copy-start(f32[16,32]{1,0:T(8,128)} %get-tuple-element.1021) | copy-start | bytes 6148
  78.9 11.1 %copy-start.194 = (f32[16,992]{1,0:T(8,128)S(1)}, f32[16,992]{1,0:T(8,128)}, u32[]{:S(2)}) copy-start(f32[16,992]{1,0:T(8,128)} %get-tuple-element.1025) | copy-start | bytes 190468
  78.9 11.1 %copy-start.350 = (f32[16,32]{1,0:T(8,128)S(1)}, f32[16,32]{1,0:T(8,128)}, u32[]{:S(2)}) copy-start(f32[16,32]{1,0:T(8,128)} %get-tuple-element.1027) | copy-start | bytes 6148
  79.1 11.0 %copy-start.197 = (f32[16,1023]{1,0:T(8,128)S(1)}, f32[16,1023]{1,0:T(8,128)}, u32[]{:S(2)}) copy-start(f32[16,1023]{1,0:T(8,128)} %get-tuple-element.1031) | copy-start | bytes 196420
  79.1 11.0 %copy-start.353 = (f32[16,1]{1,0:T(8,128)S(1)}, f32[16,1]{1,0:T(8,128)}, u32[]{:S(2)}) copy-start(f32[16,1]{1,0:T(8,128)} %get-tuple-element.1029) | copy-start | bytes 196
  79.1 11.0 %copy-start.200 = (f32[16,1023]{1,0:T(8,128)S(1)}, f32[16,1023]{1,0:T(8,128)}, u32[]{:S(2)}) copy-start(f32[16,1023]{1,0:T(8,128)} %get-tuple-element.1033) | copy-start | bytes 196420
  79.1 11.0 %copy-start.356 = (f32[16,1]{1,0:T(8,128)S(1)}, f32[16,1]{1,0:T(8,128)}, u32[]{:S(2)}) copy-start(f32[16,1]{1,0:T(8,128)} %get-tuple-element.1035) | copy-start | bytes 196
  79.5 10.8 %copy-start.203 = (f32[16,991]{1,0:T(8,128)S(1)}, f32[16,991]{1,0:T(8,128)}, u32[]{:S(2)}) copy-start(f32[16,991]{1,0:T(8,128)} %get-tuple-element.1071) | copy-start | bytes 190276
  79.5 10.8 %copy-start.359 = (f32[16,33]{1,0:T(8,128)S(1)}, f32[16,33]{1,0:T(8,128)}, u32[]{:S(2)}) copy-start(f32[16,33]{1,0:T(8,128)} %get-tuple-element.1069) | copy-start | bytes 6340
  79.5 10.8 %copy-start.206 = (f32[16,991]{1,0:T(8,128)S(1)}, f32[16,991]{1,0:T(8,128)}, u32[]{:S(2)}) copy-start(f32[16,991]{1,0:T(8,128)} %get-tuple-element.1073) | copy-start | bytes 190276
  79.5 10.8 %copy-start.362 = (f32[16,33]{1,0:T(8,128)S(1)}, f32[16,33]{1,0:T(8,128)}, u32[]{:S(2)}) copy-start(f32[16,33]{1,0:T(8,128)} %get-tuple-element.1075) | copy-start | bytes 6340
  80.4 21.0 %all-to-all-start = ((f32[16,1,2880]{2,1,0:T(1,128)}), f32[16,1,2880]{2,1,0:T(1,128)S(1)}, u32[]{:S(2)}, u32[]{:S(2)}) async-start(f32[16,1,2880]{2,1,0:T(1,128)} %copy.680), calls=%async_computation | async-start | bytes 376832 | tf_op jit(solution)/shard_map/all_to_all | solution.py:152
  90.4 10.9 %copy-start.2 = (f32[19,16,1024]{2,1,0:T(8,128)S(1)}, f32[19,16,1024]{2,1,0:T(8,128)}, u32[]{:S(2)}) copy-start(f32[19,16,1024]{2,1,0:T(8,128)} %get-tuple-element.745) | copy-start | bytes 3735556
  90.4 10.9 %copy-start.77 = (f32[1,16,1024]{2,1,0:T(8,128)S(1)}, f32[1,16,1024]{2,1,0:T(8,128)}, u32[]{:S(2)}) copy-start(f32[1,16,1024]{2,1,0:T(8,128)} %get-tuple-element.702) | copy-start | bytes 196612
  90.5 10.9 %copy-start.75 = (f32[1,16,1024]{2,1,0:T(8,128)S(1)}, f32[1,16,1024]{2,1,0:T(8,128)}, u32[]{:S(2)}) copy-start(f32[1,16,1024]{2,1,0:T(8,128)} %get-tuple-element.701) | copy-start | bytes 196612
  154.8 5.0 collective-permute-start.2
  154.8 4.1 collective-permute-start.3
  210.0 19.7 %all-to-all-start.1 = ((f32[16,1,2880]{2,1,0:T(1,128)}), f32[16,1,2880]{2,1,0:T(1,128)S(1)}, u32[]{:S(2)}, u32[]{:S(2)}) async-start(f32[16,1,2880]{2,1,0:T(1,128)} %copy.703), calls=%async_computation.1 | async-start | bytes 376832 | tf_op jit(solution)/shard_map/all_to_all | solution.py:152
  218.7 11.0 %copy-start.3 = (f32[19,16,1024]{2,1,0:T(8,128)S(1)}, f32[19,16,1024]{2,1,0:T(8,128)}, u32[]{:S(2)}) copy-start(f32[19,16,1024]{2,1,0:T(8,128)} %get-tuple-element.735) | copy-start | bytes 3735556
  218.7 11.0 %copy-start.81 = (f32[1,16,1024]{2,1,0:T(8,128)S(1)}, f32[1,16,1024]{2,1,0:T(8,128)}, u32[]{:S(2)}) copy-start(f32[1,16,1024]{2,1,0:T(8,128)} %get-tuple-element.692) | copy-start | bytes 196612
  218.8 10.9 %copy-start.79 = (f32[1,16,1024]{2,1,0:T(8,128)S(1)}, f32[1,16,1024]{2,1,0:T(8,128)}, u32[]{:S(2)}) copy-start(f32[1,16,1024]{2,1,0:T(8,128)} %get-tuple-element.691) | copy-start | bytes 196612
  265.9 10.6 %copy-start.22 = (f32[1,16,1023]{2,1,0:T(8,128)S(1)}, f32[1,16,1023]{2,1,0:T(8,128)}, u32[]{:S(2)}) copy-start(f32[1,16,1023]{2,1,0:T(8,128)} %get-tuple-element.940) | copy-start | bytes 196420
  283.3 4.9 collective-permute-start.4
  283.3 4.1 collective-permute-start.5
  338.1 19.9 %all-to-all-start.2 = ((f32[16,1,2880]{2,1,0:T(1,128)}), f32[16,1,2880]{2,1,0:T(1,128)S(1)}, u32[]{:S(2)}, u32[]{:S(2)}) async-start(f32[16,1,2880]{2,1,0:T(1,128)} %copy.726), calls=%async_computation.2 | async-start | bytes 376832 | tf_op jit(solution)/shard_map/all_to_all | solution.py:152
  347.0 11.0 %copy-start.4 = (f32[19,16,1024]{2,1,0:T(8,128)S(1)}, f32[19,16,1024]{2,1,0:T(8,128)}, u32[]{:S(2)}) copy-start(f32[19,16,1024]{2,1,0:T(8,128)} %get-tuple-element.725) | copy-start | bytes 3735556
  347.0 11.0 %copy-start.85 = (f32[1,16,1024]{2,1,0:T(8,128)S(1)}, f32[1,16,1024]{2,1,0:T(8,128)}, u32[]{:S(2)}) copy-start(f32[1,16,1024]{2,1,0:T(8,128)} %get-tuple-element.682) | copy-start | bytes 196612
  347.1 10.9 %copy-start.83 = (f32[1,16,1024]{2,1,0:T(8,128)S(1)}, f32[1,16,1024]{2,1,0:T(8,128)}, u32[]{:S(2)}) copy-start(f32[1,16,1024]{2,1,0:T(8,128)} %get-tuple-element.681) | copy-start | bytes 196612
  394.2 10.6 %copy-start.23 = (f32[1,16,1023]{2,1,0:T(8,128)S(1)}, f32[1,16,1023]{2,1,0:T(8,128)}, u32[]{:S(2)}) copy-start(f32[1,16,1023]{2,1,0:T(8,128)} %get-tuple-element.1004) | copy-start | bytes 196420
  411.5 5.0 collective-permute-start.6
  411.5 4.1 collective-permute-start.7
  451.9 10.9 %copy-start.183 = (f32[2,8,8,128]{3,2,1,0:T(8,128)S(1)}, f32[2,8,8,128]{3,2,1,0:T(8,128)}, u32[]{:S(2)}) copy-start(f32[2,8,8,128]{3,2,1,0:T(8,128)} %get-tuple-element.670) | copy-start | bytes 196612
  452.0 10.8 %copy-start.182 = (f32[1,16,1024]{2,1,0:T(8,128)S(1)}, f32[1,16,1024]{2,1,0:T(8,128)}, u32[]{:S(2)}) copy-start(f32[1,16,1024]{2,1,0:T(8,128)} %get-tuple-element.671) | copy-start | bytes 196612
  454.3 20.2 %copy-start.404 = (pred[8]{0:T(512)(128)(4,1)S(1)}, pred[8]{0:T(512)(128)(4,1)}, u32[]{:S(2)}) copy-start(pred[8]{0:T(512)(128)(4,1)} %get-tuple-element.651) | copy-start | bytes 28
  454.3 15.6 %all-to-all-start.3 = ((f32[16,1,2880]{2,1,0:T(1,128)}), f32[16,1,2880]{2,1,0:T(1,128)S(1)}, u32[]{:S(2)}, u32[]{:S(2)}) async-start(f32[16,1,2880]{2,1,0:T(1,128)} %copy.749), calls=%async_computation.3 | async-start | bytes 376832 | tf_op jit(solution)/shard_map/all_to_all | solution.py:152
  462.2 12.6 %copy-start.414 = (s32[5]{0:T(128)S(1)}, s32[5]{0:T(128)}, u32[]{:S(2)}) copy-start(s32[5]{0:T(128)} %constant.1290) | copy-start | bytes 64
  469.9 35.5 %all-to-all-start.5 = ((s32[16,1,8]{2,1,0:T(1,128)}), s32[16,1,8]{2,1,0:T(1,128)S(1)}, u32[]{:S(2)}, u32[]{:S(2)}) async-start(s32[16,1,8]{2,1,0:T(1,128)} %bitcast.352), calls=%async_computation.5 | async-start | bytes 16384 | tf_op jit(solution)/shard_map/all_to_all | solution.py:320
  503.1 17.4 %copy-start.370 = (bf16[256,64]{0,1:T(8,128)(2,1)S(1)}, bf16[256,64]{0,1:T(8,128)(2,1)}, u32[]{:S(2)}) copy-start(bf16[256,64]{0,1:T(8,128)(2,1)} %get-tuple-element.1085) | copy-start | bytes 98308
  503.1 17.3 %copy-start.371 = (bf16[256,64]{0,1:T(8,128)(2,1)S(1)}, bf16[256,64]{0,1:T(8,128)(2,1)}, u32[]{:S(2)}) copy-start(bf16[256,64]{0,1:T(8,128)(2,1)} %get-tuple-element.1086) | copy-start | bytes 98308
  503.5 19.2 %copy-start.265 = (f32[3,512]{1,0:T(4,128)S(1)}, f32[3,512]{1,0:T(4,128)}, u32[]{:S(2)}) copy-start(f32[3,512]{1,0:T(4,128)} %param.149) | copy-start | bytes 18436
  503.6 19.2 %copy-start.307 = (bf16[128,3]{0,1:T(4,128)(2,1)S(1)}, bf16[128,3]{0,1:T(4,128)(2,1)}, u32[]{:S(2)}) copy-start(bf16[128,3]{0,1:T(4,128)(2,1)} %reshape.9282) | copy-start | bytes 2308
  505.4 14.8 %all-to-all-start.4 = ((bf16[16,8,512]{2,1,0:T(8,128)(2,1)}), bf16[16,8,512]{2,1,0:T(8,128)(2,1)S(1)}, u32[]{:S(2)}, u32[]{:S(2)}) async-start(bf16[16,8,512]{2,1,0:T(8,128)(2,1)} %bitcast_select_fusion), calls=%async_computation.4 | async-start | bytes 262144 | tf_op jit(solution)/shard_map/all_to_all | solution.py:319
  512.4 154.9 %reduce-scatter.2.cloned.1.call-start = ((), (), s32[]{:S(2)}) async-start(), calls=%async_computation.7 | async-start | bytes 278528 | tf_op jit(solution)/shard_map/reduce_scatter | solution.py:334
  (383 other events, 2117.6 us)
Sparse Core Ops, SparseCore 0:
  593.0 74.2 reduce-scatter.1
where the time goes:
time: 686 us; the launch traced here: 674 us
  local copies, waits for them, and re-layouts  359 us (52%)
  other arithmetic  153 us (22%)
  waiting for transfers between devices  87.7 us (13%)
  starting transfers between devices  43.9 us (6%)
  between operations  22.9 us (3%)
    reduce_scatter x1, waiting for transfers between devices, body(): lax.psum_scatter(partial_value, 'blk', scatter_dimension=0, tiled=True)  74.4 us
    reduce_sum x4, other arithmetic, radiate(): real_part = jnp.sum(weight_real * cosine + weight_imag * sine_part, axis=0)  67.3 us
    slice x96, local copies, waits for them, and re-layouts, stream_merged(): jnp.roll(widened[number, begin:begin + slab_depth], shift_y * BS + shift_...  63.9 us
    unnamed x110, other arithmetic  53.2 us
    concatenate x8, local copies, waits for them, and re-layouts, body(): widened = jnp.concatenate([lower_plane, collided, upper_plane], axis=1)  50.4 us
    another operation x120, local copies, waits for them, and re-layouts, stream_merged(): jnp.tile(row_values, (1, BS))  48.2 us
    reshape x80, local copies, waits for them, and re-layouts, stream_merged(): jnp.repeat(column_values, BS, axis=-1)  47.6 us
    unnamed x979, local copies, waits for them, and re-layouts  44.4 us
  transfers between devices with their start and end apart: 15, of which 3 were waited for; matrix products, arithmetic and copies ran while one was open for 14% of the time, Pallas kernels for 0%

commit v1 on v0

v1 whole, which is shorter than its diff:
```python
import math

import jax
import jax.numpy as jnp
from jax import lax
from jax.experimental import pallas as pl
from jax.experimental.pallas import tpu as pltpu
from jax.sharding import PartitionSpec as P

BS = 32
STEPS = 4
SAMPLES = 256
BINS = 64
P_OWN = 64


velocity_list = [
    (0, 0, 0),
    (1, 0, 0),
    (-1, 0, 0),
    (0, 1, 0),
    (0, -1, 0),
    (0, 0, 1),
    (0, 0, -1),
    (1, 1, 0),
    (-1, -1, 0),
    (1, -1, 0),
    (-1, 1, 0),
    (1, 0, 1),
    (-1, 0, -1),
    (1, 0, -1),
    (-1, 0, 1),
    (0, 1, 1),
    (0, -1, -1),
    (0, 1, -1),
    (0, -1, 1),
]
weight_list = [1.0 / 3.0] + [1.0 / 18.0] * 6 + [1.0 / 36.0] * 12
x_moving = [1, 2, 7, 8, 9, 10, 11, 12, 13, 14]
y_upward = [3, 7, 10, 15, 17]
y_downward = [4, 8, 9, 16, 18]
z_upward = [5, 11, 14, 15, 18]
z_downward = [6, 12, 13, 16, 17]
relax_rate = 1.6
pressure_gain = 60.0
sound_speed = 0.5


x_plus = [1, 7, 9, 11, 13]
x_minus = [2, 8, 10, 12, 14]
x_order = x_plus + x_minus
still = [0, 3, 4, 5, 6, 15, 16, 17, 18]
LANES = 128
FACE = 256


def collide_tile(f):
    density = f[0]
    for part in f[1:]:
        density = density + part
    speeds = []
    for axis in range(3):
        plus = None
        minus = None
        for number, velocity in enumerate(velocity_list):
            if velocity[axis] == 1:
                plus = f[number] if plus is None else plus + f[number]
            elif velocity[axis] == -1:
                minus = f[number] if minus is None else minus + f[number]
        speeds.append(plus - minus)
    inverse = 1.0 / density
    speeds = [speed * inverse for speed in speeds]
    squared = speeds[0] * speeds[0] + speeds[1] * speeds[1] + speeds[2] * speeds[2]
    base = 1.0 - 1.5 * squared
    scaled = {}
    for weight in sorted(set(weight_list)):
        scaled[weight] = (relax_rate * weight) * density
    out = []
    for number, velocity in enumerate(velocity_list):
        projected = None
        for axis in range(3):
            if velocity[axis] == 0:
                continue
            if projected is None:
                projected = speeds[axis] if velocity[axis] == 1 else -speeds[axis]
            elif velocity[axis] == 1:
                projected = projected + speeds[axis]
            else:
                projected = projected - speeds[axis]
        bracket = base
        if projected is not None:
            bracket = base + projected * (3.0 + 4.5 * projected)
        out.append((1.0 - relax_rate) * f[number] + scaled[weight_list[number]] * bracket)
    return out, density


def emit_collided(load, still_ref, moving_ref, up_ref, down_ref, density_ref):
    depth = still_ref.shape[1]
    for tile in range(still_ref.shape[2] // LANES):
        lanes = slice(tile * LANES, (tile + 1) * LANES)
        out, density = collide_tile([load(number, lanes) for number in range(19)])
        for place, number in enumerate(still):
            still_ref[place, :, lanes] = out[number]
        for place, number in enumerate(x_order):
            moving_ref[place, :, lanes] = out[number]
        for place, number in enumerate(x_plus):
            up_ref[place, :, lanes] = out[number][depth - 1 : depth]
        for place, number in enumerate(x_minus):
            down_ref[place, :, lanes] = out[number][0:1]
        if density_ref is not None:
            density_ref[:, lanes] = density


def first_kernel(field_ref, still_ref, moving_ref, up_ref, down_ref):
    emit_collided(
        lambda number, lanes: field_ref[number, :, lanes],
        still_ref, moving_ref, up_ref, down_ref, None,
    )


def lane_of(shape):
    return lax.broadcasted_iota(jnp.int32, shape, 1)


def turned(value, amount):
    amount = amount % value.shape[1]
    return value if amount == 0 else pltpu.roll(value, amount, 1)


def pack_kernel(target_ref, still_ref, moving_ref, low_ref, high_ref, shifted_ref, message_ref):
    depth = still_ref.shape[1]
    count = still_ref.shape[2]
    for place in range(5):
        shifted_ref[place, 0:1, :] = low_ref[place]
        shifted_ref[place, 1:depth, :] = moving_ref[place, 0 : depth - 1, :]
        shifted_ref[place + 5, depth - 1 : depth, :] = high_ref[place]
        shifted_ref[place + 5, 0 : depth - 1, :] = moving_ref[place + 5, 1:depth, :]

    def load(number, lanes):
        if number in still:
            return still_ref[still.index(number), :, lanes]
        return shifted_ref[x_order.index(number), :, lanes]

    small = lane_of((depth, LANES))
    wide = lane_of((depth, count)) % BS
    first = slice(0, LANES)
    last = slice(count - LANES, count)
    for piece, (chosen, lanes, begin) in enumerate(
        [(y_downward, first, 0), (y_upward, last, LANES - BS)]
    ):
        packed = jnp.zeros((depth, LANES), jnp.float32)
        for j in range(4):
            moved = turned(load(chosen[j], lanes), j * BS - begin)
            packed = jnp.where(small // BS == j, moved, packed)
        message_ref[target_ref[piece], :, 0:LANES] = packed
        message_ref[target_ref[piece], :, LANES:FACE] = turned(load(chosen[4], lanes), -begin)
    for piece, (chosen, begin) in enumerate([(z_downward, 0), (z_upward, BS - 1)]):
        gathered = jnp.zeros((depth, count), jnp.float32)
        for j in range(5):
            moved = turned(load(chosen[j], slice(0, count)), j - begin)
            gathered = jnp.where(wide == j, moved, gathered)
        for half in range(2):
            packed = jnp.zeros((depth, LANES), jnp.float32)
            for u in range(4):
                tile = half * 4 + u
                moved = turned(gathered[:, tile * LANES : (tile + 1) * LANES], 8 * u)
                packed = jnp.where(small % BS // 8 == u, moved, packed)
            message_ref[target_ref[2 + piece], :, half * LANES : (half + 1) * LANES] = packed
    for piece, (number, lanes) in enumerate([(16, first), (18, first), (17, last), (15, last)]):
        message_ref[target_ref[4 + piece], :, 0:LANES] = load(number, lanes)


def stream_into(target_ref, still_ref, shifted_ref, message_ref, out_ref):
    depth = still_ref.shape[1]
    count = still_ref.shape[2]
    small = lane_of((depth, LANES))
    wide = lane_of((depth, count)) % BS
    columns = []
    for piece in range(2):
        tiles = []
        for half in range(2):
            packed = message_ref[target_ref[2 + piece], :, half * LANES : (half + 1) * LANES]
            tiles += [turned(packed, -8 * u) for u in range(4)]
        columns.append(jnp.concatenate(tiles, axis=1))
    corners = {15: (4, 0, 127), 17: (5, 31, 96), 18: (6, 96, 31), 16: (7, 127, 0)}
    for number, (shift_x, shift_y, shift_z) in enumerate(velocity_list):
        if number in still:
            value = still_ref[still.index(number)]
        else:
            value = shifted_ref[x_order.index(number)]
        value = turned(value, shift_y * BS + shift_z)
        if shift_z != 0:
            chosen, piece, edge = (z_upward, 0, 0) if shift_z == 1 else (z_downward, 1, BS - 1)
            column = turned(columns[piece], edge - chosen.index(number) + BS * shift_y)
            value = jnp.where(wide == edge, column, value)
        out_ref[number] = value
        if shift_y != 0:
            chosen, piece, lanes, edge = (
                (y_upward, 0, slice(0, LANES), 0)
                if shift_y == 1
                else (y_downward, 1, slice(count - LANES, count), LANES - BS)
            )
            j = chosen.index(number)
            begin = j // 4 * LANES
            row = message_ref[target_ref[piece], :, begin : begin + LANES]
            row = turned(row, edge - j % 4 * BS + shift_z)
            keep = small // BS == edge // BS
            if shift_z != 0:
                keep = keep & (small % BS != (0 if shift_z == 1 else BS - 1))
            old = value[:, lanes]
            fixed = jnp.where(keep, row, old)
            if number in corners:
                slot, lane_to, lane_from = corners[number]
                corner = turned(message_ref[target_ref[slot], :, 0:LANES], lane_to - lane_from)
                fixed = jnp.where(small == lane_to, corner, fixed)
            out_ref[number, :, lanes] = fixed


def middle_kernel(
    target_ref, still_in, shifted_in, message_ref,
    still_ref, moving_ref, up_ref, down_ref, density_ref, field_ref,
):
    stream_into(target_ref, still_in, shifted_in, message_ref, field_ref)
    emit_collided(
        lambda number, lanes: field_ref[number, :, lanes],
        still_ref, moving_ref, up_ref, down_ref, density_ref,
    )


def last_kernel(target_ref, still_in, shifted_in, message_ref, field_ref, density_ref):
    stream_into(target_ref, still_in, shifted_in, message_ref, field_ref)
    total = field_ref[0]
    for number in range(1, 19):
        total = total + field_ref[number]
    density_ref[...] = total


def call(kernel, outs, scalars, *arrays, scratch=()):
    vmem = pl.BlockSpec(memory_space=pltpu.VMEM)
    smem = pl.BlockSpec(memory_space=pltpu.SMEM)
    shapes = [jax.ShapeDtypeStruct(shape, jnp.float32) for shape in outs]
    return pl.pallas_call(
        kernel,
        out_shape=shapes,
        in_specs=[smem] * len(scalars) + [vmem] * len(arrays),
        out_specs=[vmem] * len(outs),
        scratch_shapes=[pltpu.VMEM(shape, jnp.float32) for shape in scratch],
    )(*scalars, *arrays)


def transform_table():
    moments = jnp.arange(SAMPLES, dtype=jnp.int32)[:, None]
    harmonics = jnp.arange(BINS, dtype=jnp.int32)[None, :] + 1
    turns = moments * harmonics % SAMPLES
    phases = turns.astype(jnp.float32) * (2.0 * math.pi / SAMPLES)
    return jnp.concatenate([jnp.cos(phases), -jnp.sin(phases)], axis=1).astype(jnp.bfloat16)


def radiate_kernel(panel_ref, listen_ref, out_ref, real_ref, imag_ref):
    listeners = listen_ref.shape[1]
    real_ref[...] = jnp.zeros_like(real_ref)
    imag_ref[...] = jnp.zeros_like(imag_ref)
    step_angle = 2.0 * math.pi / SAMPLES / sound_speed

    def accumulate(block_number, carry):
        begin = pl.multiple_of(block_number * 8, 8)
        panel = panel_ref[pl.ds(begin, 8), :]
        distance_sq = None
        facing = None
        for axis in range(3):
            at = 4 * BINS + axis
            offset = listen_ref[axis : axis + 1, :] - panel[:, at : at + 1]
            square = offset * offset
            along = panel[:, at + 3 : at + 4] * offset
            distance_sq = square if distance_sq is None else distance_sq + square
            facing = along if facing is None else facing + along
        distance = jnp.sqrt(distance_sq)
        far_term = facing / (4.0 * math.pi * sound_speed * distance_sq)
        ratio = sound_speed / distance
        angle = step_angle * distance
        turn_cos = jnp.cos(angle)
        turn_sin = jnp.sin(angle)
        wave_cos = far_term * turn_cos
        wave_sin = far_term * turn_sin
        for k in range(BINS):
            press_real = panel[:, k : k + 1]
            press_imag = panel[:, BINS + k : BINS + k + 1]
            rate_real = panel[:, 2 * BINS + k : 2 * BINS + k + 1]
            rate_imag = panel[:, 3 * BINS + k : 3 * BINS + k + 1]
            mixed_real = rate_real + ratio * press_real
            mixed_imag = rate_imag + ratio * press_imag
            real_ref[k] += mixed_real * wave_cos + mixed_imag * wave_sin
            imag_ref[k] += mixed_imag * wave_cos - mixed_real * wave_sin
            if k + 1 < BINS:
                wave_cos, wave_sin = (
                    wave_cos * turn_cos - wave_sin * turn_sin,
                    wave_sin * turn_cos + wave_cos * turn_sin,
                )
        return carry

    lax.fori_loop(0, panel_ref.shape[0] // 8, accumulate, 0)
    both = jnp.concatenate([jnp.sum(real_ref[...], axis=1), jnp.sum(imag_ref[...], axis=1)], axis=0)
    out_ref[...] = both.T


def route_slots(payload, owners, alive_slot, blocks):
    count_slots = payload.shape[0]
    capacity = -(-count_slots // blocks)
    target = owners // P_OWN
    member = (
        (target[:, None] == jnp.arange(blocks, dtype=jnp.int32)[None, :]) & alive_slot[:, None]
    ).astype(jnp.int32)
    before = jnp.cumsum(member, axis=0) - member
    order_within = jnp.sum(before * member, axis=1)
    slot_label = jnp.where(alive_slot, target * capacity + order_within, -1)
    matches = slot_label[:, None] == jnp.arange(blocks * capacity, dtype=jnp.int32)[None, :]
    source = jnp.sum(
        jnp.where(matches, jnp.arange(count_slots, dtype=jnp.int32)[:, None], 0), axis=0
    )
    filled = jnp.any(matches, axis=0)
    outgoing = jnp.take(payload, source, axis=0).reshape(blocks, capacity, payload.shape[1])
    spots = jnp.where(filled, jnp.take(owners, source) % P_OWN, -1).reshape(blocks, capacity, 1)
    return jnp.concatenate([outgoing, spots.astype(jnp.bfloat16)], axis=2)


def settle(incoming):
    width = incoming.shape[-1] - 1
    flat = incoming.reshape(-1, width + 1)
    spots = flat[:, width].astype(jnp.int32)
    choose = (spots[:, None] == jnp.arange(P_OWN, dtype=jnp.int32)[None, :]).astype(jnp.bfloat16)
    return jnp.einsum(
        "rp,rw->pw", choose, flat[:, :width], preferred_element_type=jnp.float32
    ).astype(jnp.bfloat16)


def body(
    populations,
    block_faces,
    block_edges,
    probe_cell,
    history,
    panel_count,
    panel_owner,
    panel_pos,
    panel_normal,
    observers,
):
    blocks = lax.axis_size("blk")
    lattice_state = populations[0]
    slab_depth = lattice_state.shape[1]
    lane_count = lattice_state.shape[2]
    targets = jnp.concatenate([block_faces[0], block_edges[0]])
    ring = lax.axis_size("obs")
    forward = [(i, (i + 1) % ring) for i in range(ring)]
    backward = [(target, source) for source, target in forward]
    still_shape = (len(still), slab_depth, lane_count)
    moving_shape = (len(x_order), slab_depth, lane_count)
    edge_shape = (5, 1, lane_count)
    collided_shapes = [still_shape, moving_shape, edge_shape, edge_shape]
    plane_shape = (slab_depth, lane_count)
    field_shape = (19, slab_depth, lane_count)
    still_part, moving_part, up, down = call(first_kernel, collided_shapes, (), lattice_state)
    densities = []
    for turn_index in range(STEPS):
        low = lax.ppermute(up, "obs", forward)
        high = lax.ppermute(down, "obs", backward)
        shifted, outgoing = call(
            pack_kernel,
            [moving_shape, (blocks, slab_depth, FACE)],
            (targets,), still_part, moving_part, low, high,
        )
        received = lax.all_to_all(outgoing, "blk", split_axis=0, concat_axis=0, tiled=True)
        if turn_index + 1 < STEPS:
            still_part, moving_part, up, down, density = call(
                middle_kernel,
                collided_shapes + [plane_shape],
                (targets,), still_part, shifted, received,
                scratch=[field_shape],
            )
        else:
            lattice_state, density = call(
                last_kernel, [field_shape, plane_shape], (targets,), still_part, shifted, received
            )
        densities.append(density)
    populations_out = lattice_state.reshape(1, 19, slab_depth, lane_count)
    readings = [jnp.take(density.reshape(-1), probe_cell) for density in densities]
    gained = pressure_gain * (jnp.stack(readings, axis=1) - 1.0)
    previous = jnp.concatenate(
        [history[:, SAMPLES - 1 : SAMPLES].astype(jnp.float32), gained[:, :-1]], axis=1
    )
    rate_values = gained - previous
    recent = jnp.concatenate(
        [
            history[:, STEPS:SAMPLES],
            gained.astype(jnp.bfloat16),
            history[:, SAMPLES + STEPS :],
            rate_values.astype(jnp.bfloat16),
        ],
        axis=1,
    )
    transform = transform_table()
    count_slots = recent.shape[0]
    alive_slot = jnp.arange(count_slots, dtype=jnp.int32) < panel_count[0]
    outgoing = route_slots(recent, panel_owner, alive_slot, blocks)
    incoming = lax.all_to_all(outgoing, "blk", split_axis=0, concat_axis=0, tiled=True)
    owned = settle(incoming).reshape(P_OWN, 2, SAMPLES)
    spectra = (
        jnp.einsum("pgt,tk->pgk", owned, transform, preferred_element_type=jnp.float32)
        .astype(jnp.bfloat16)
        .reshape(P_OWN, 4 * BINS)
    )
    panels = jnp.concatenate([spectra, panel_pos.T, panel_normal.T], axis=1)
    gathered = lax.all_gather(panels, "obs", axis=0, tiled=True).astype(jnp.float32)
    listeners = observers.shape[1]
    partial_value = call(
        radiate_kernel,
        [(listeners, 2 * BINS)],
        (), gathered, observers,
        scratch=[(BINS, 8, listeners), (BINS, 8, listeners)],
    )[0]
    pieces = lax.all_to_all(
        partial_value.reshape(blocks, listeners // blocks, 2 * BINS),
        "blk", split_axis=0, concat_axis=0, tiled=True,
    )
    return (populations_out, jnp.sum(pieces, axis=0)[None])


def solution(mesh):
    placed = (
        P("blk", None, "obs", None),
        P("blk", None),
        P("blk", None),
        P(("blk", "obs")),
        P(("blk", "obs"), None),
        P(("blk", "obs")),
        P(("blk", "obs")),
        P(None, ("blk", "obs")),
        P(None, ("blk", "obs")),
        P(None, "obs"),
    )
    return jax.shard_map(
        body,
        mesh=mesh,
        in_specs=placed,
        out_specs=(P("blk", None, "obs", None), P("obs", "blk", None)),
        check_vma=False,
    )
```

time: 686 us -> 150 us (0.22); the launches traced: 674 us -> 149 us
  local copies, waits for them, and re-layouts: 359 us -> 14.3 us
  other arithmetic: 153 us -> 4.08 us
  Pallas kernels: 0 us -> 42.4 us
  waiting for transfers between devices: 87.7 us -> 45.9 us
  between operations: 22.9 us -> 1.69 us
  starting transfers between devices: 43.9 us -> 24.7 us
  blocking collectives: 5.8 us -> 15.8 us
    reduce_sum x17 -> x1, other arithmetic: 75.4 us -> 0.63 us  [body(): return (populations_out, jnp.sum(pieces, axis=0)[None])]
    reduce_scatter x1 -> x0, waiting for transfers between devices: 74.4 us -> none  [body(): lax.psum_scatter(partial_value, 'blk', scatter_dimension=0, tiled=True)]
    slice x124 -> x0, local copies, waits for them, and re-layouts: 68.6 us -> none  [the longest x96 63.9 us: stream_merged(): jnp.roll(widened[number, begin:begin + slab_depth], shift_y * BS + shift_...]
    concatenate x28 -> x0, local copies, waits for them, and re-layouts: 62.6 us -> none  [the longest x8 50.4 us: body(): widened = jnp.concatenate([lower_plane, collided, upper_plane], axis=1)]
    unnamed x110 -> x0, other arithmetic: 53.2 us -> none
    another operation x176 -> x0, local copies, waits for them, and re-layouts: 52 us -> none  [the longest x120 48.2 us: stream_merged(): jnp.tile(row_values, (1, BS))]
    reshape x85 -> x1, local copies, waits for them, and re-layouts: 48.2 us -> 0.01 us  [body(): spectra = jnp.einsum('pgt,tk->pgk', owned, transform, preferred_element_t...]
    gather x46 -> x7, local copies, waits for them, and re-layouts: 51 us -> 5.99 us  [the longest x4 4.59 us: body(): jnp.take(density.reshape(-1), probe_cell)]
  transfers between devices with their start and end apart: 15 -> 13, of which waited for: 3 -> 12; matrix products, arithmetic and copies ran while one was open for 14% -> 5% of each run, Pallas kernels for 0% -> 0%
where the time goes in v1:
time: 150 us; the launch traced here: 149 us
  waiting for transfers between devices  45.9 us (31%)
  Pallas kernels  42.4 us (28%)
  starting transfers between devices  24.7 us (16%)
  blocking collectives  15.8 us (11%)
  local copies, waits for them, and re-layouts  14.3 us (10%)
  other arithmetic  4.08 us (3%)
  between operations  1.69 us (1%)
    all_to_all x5, waiting for transfers between devices, body(): lax.all_to_all(outgoing, 'blk', split_axis=0, concat_axis=0, tiled=True)  42.9 us
    pallas_call x10, Pallas kernels, call(): pl.pallas_call(kernel, out_shape=shapes, in_specs=[smem] * len(scalars) +...  42.4 us
    all_to_all x5, starting transfers between devices, body(): lax.all_to_all(outgoing, 'blk', split_axis=0, concat_axis=0, tiled=True)  22.6 us
    all_to_all x1, blocking collectives, body(): lax.all_to_all(partial_value.reshape(blocks, listeners // blocks, 2 * BIN...  13.9 us
    unnamed x51, local copies, waits for them, and re-layouts  6.47 us
    gather x4, local copies, waits for them, and re-layouts, body(): jnp.take(density.reshape(-1), probe_cell)  4.59 us
  transfers between devices with their start and end apart: 13, of which 12 were waited for; matrix products, arithmetic and copies ran while one was open for 5% of the time, Pallas kernels for 0%

profile of v1, /device:TPU:0, one launch (start us, length us, event | category | flops | bytes accessed | tf_op | source)
XLA Modules:
  0.0 149.4 jit_solution(17287873246640119486)
XLA Ops:
  0.7 2.8 %shard_map.113 = (f32[9,16,1024]{2,1,0:T(8,128)}, f32[10,16,1024]{2,1,0:T(8,128)}, f32[5,1,1024]{2,1,0:T(1,128)}, f32[5,1,1024]{2,1,0:T(1,128)}) custom-call(f32[19,16,1024]{2,1,0:T(8,128)} %bitcast.51), custom_call_target="tpu_custom_call" | custom-call | tf_op jit(solution)/shard_map/pallas_call | solution.py:242
  3.4 0.5 collective-permute-start
  3.9 0.6 pad_add_fusion.target_ref
  5.2 0.1 collective-permute-done.1.high_ref
  5.3 0.5 copy-done.10
  5.8 0.1 copy-done.14
  5.9 2.6 %shard_map.114 = (f32[10,16,1024]{2,1,0:T(8,128)}, f32[16,16,256]{2,1,0:T(8,128)}) custom-call(s32[8]{0:T(128)} %pad_add_fusion.target_ref, f32[9,16,1024]{2,1,0:T(8,128)} %get-tuple-element.32.still_ref.still_in, f32[10,16,1024]{2,1,0:T(8,128)} %get-tuple-element.33.moving_ref, f32[5,1,1024]{2,1,0:T(1,128)} %copy-done.10, f32[5,1,1024]{2,1,0:T(1,128)} %copy-done.14), custom_call_target="tpu_custom_call" | custom-call | tf_op jit(solution)/shard_map/pallas_call | solution.py:242
  8.5 8.2 %all-to-all-start = ((f32[16,16,256]{2,1,0:T(8,128)}), f32[16,16,256]{2,1,0:T(8,128)S(1)}, u32[]{:S(2)}, u32[]{:S(2)}) async-start(f32[16,16,256]{2,1,0:T(8,128)} %get-tuple-element.37), calls=%async_computation | async-start | bytes 524288 | tf_op jit(solution)/shard_map/all_to_all | solution.py:372
  16.8 0.2 reduce_window_sum.11
  17.0 9.8 %all-to-all-done.message_ref = f32[16,16,256]{2,1,0:T(8,128)S(1)} async-done(((f32[16,16,256]{2,1,0:T(8,128)}), f32[16,16,256]{2,1,0:T(8,128)S(1)}, u32[]{:S(2)}, u32[]{:S(2)}) %all-to-all-start) | async-done | bytes 262176 | tf_op jit(solution)/shard_map/all_to_all | solution.py:372
  26.9 0.7 copy-done.3
  27.6 3.4 %shard_map.115 = (f32[9,16,1024]{2,1,0:T(8,128)}, f32[10,16,1024]{2,1,0:T(8,128)}, f32[5,1,1024]{2,1,0:T(1,128)}, f32[5,1,1024]{2,1,0:T(1,128)}, f32[16,1024]{1,0:T(8,128)}) custom-call(s32[8]{0:T(128)} %pad_add_fusion.target_ref, f32[9,16,1024]{2,1,0:T(8,128)} %get-tuple-element.32.still_ref.still_in, f32[10,16,1024]{2,1,0:T(8,128)} %get-tuple-element.36.shifted_in, ...), custom_call_target="tpu_custom_call" | custom-call | tf_op jit(solution)/shard_map/pallas_call | solution.py:242
  31.0 0.5 collective-permute-start.3
  31.5 0.2 select_reduce_fusion.1
  31.6 0.7 collective-permute-done.2.low_ref
  32.4 0.2 collective-permute-done.3.high_ref
  32.5 0.4 copy-done.9
  33.0 0.2 copy-done.12
  33.1 2.5 %shard_map.116 = (f32[10,16,1024]{2,1,0:T(8,128)}, f32[16,16,256]{2,1,0:T(8,128)}) custom-call(s32[8]{0:T(128)} %pad_add_fusion.target_ref, f32[9,16,1024]{2,1,0:T(8,128)} %get-tuple-element.38.still_ref.still_in, f32[10,16,1024]{2,1,0:T(8,128)} %get-tuple-element.39.moving_ref, f32[5,1,1024]{2,1,0:T(1,128)} %copy-done.9, f32[5,1,1024]{2,1,0:T(1,128)} %copy-done.12), custom_call_target="tpu_custom_call" | custom-call | tf_op jit(solution)/shard_map/pallas_call | solution.py:242
  35.7 3.5 %all-to-all-start.1 = ((f32[16,16,256]{2,1,0:T(8,128)}), f32[16,16,256]{2,1,0:T(8,128)S(1)}, u32[]{:S(2)}, u32[]{:S(2)}) async-start(f32[16,16,256]{2,1,0:T(8,128)} %get-tuple-element.43), calls=%async_computation.1 | async-start | bytes 524288 | tf_op jit(solution)/shard_map/all_to_all | solution.py:372
  39.4 10.5 %all-to-all-done.1.message_ref = f32[16,16,256]{2,1,0:T(8,128)S(1)} async-done(((f32[16,16,256]{2,1,0:T(8,128)}), f32[16,16,256]{2,1,0:T(8,128)S(1)}, u32[]{:S(2)}, u32[]{:S(2)}) %all-to-all-start.1) | async-done | bytes 262176 | tf_op jit(solution)/shard_map/all_to_all | solution.py:372
  49.8 0.7 copy-done.4
  50.5 3.4 %shard_map.117 = (f32[9,16,1024]{2,1,0:T(8,128)}, f32[10,16,1024]{2,1,0:T(8,128)}, f32[5,1,1024]{2,1,0:T(1,128)}, f32[5,1,1024]{2,1,0:T(1,128)}, f32[16,1024]{1,0:T(8,128)}) custom-call(s32[8]{0:T(128)} %pad_add_fusion.target_ref, f32[9,16,1024]{2,1,0:T(8,128)} %get-tuple-element.38.still_ref.still_in, f32[10,16,1024]{2,1,0:T(8,128)} %get-tuple-element.42.shifted_in, ...), custom_call_target="tpu_custom_call" | custom-call | tf_op jit(solution)/shard_map/pallas_call | solution.py:242
  53.9 0.5 collective-permute-start.5
  54.5 0.8 collective-permute-done.4.low_ref
  55.3 0.2 collective-permute-done.5.high_ref
  55.5 0.4 copy-done.11
  55.9 0.2 copy-done.15
  56.1 2.6 %shard_map.118 = (f32[10,16,1024]{2,1,0:T(8,128)}, f32[16,16,256]{2,1,0:T(8,128)}) custom-call(s32[8]{0:T(128)} %pad_add_fusion.target_ref, f32[9,16,1024]{2,1,0:T(8,128)} %get-tuple-element.44.still_ref.still_in, f32[10,16,1024]{2,1,0:T(8,128)} %get-tuple-element.45.moving_ref, f32[5,1,1024]{2,1,0:T(1,128)} %copy-done.11, f32[5,1,1024]{2,1,0:T(1,128)} %copy-done.15), custom_call_target="tpu_custom_call" | custom-call | tf_op jit(solution)/shard_map/pallas_call | solution.py:242
  58.7 3.7 %all-to-all-start.2 = ((f32[16,16,256]{2,1,0:T(8,128)}), f32[16,16,256]{2,1,0:T(8,128)S(1)}, u32[]{:S(2)}, u32[]{:S(2)}) async-start(f32[16,16,256]{2,1,0:T(8,128)} %get-tuple-element.49), calls=%async_computation.2 | async-start | bytes 524288 | tf_op jit(solution)/shard_map/all_to_all | solution.py:372
  62.5 1.2 gather_fusion.1
  64.2 8.7 %all-to-all-done.2.message_ref = f32[16,16,256]{2,1,0:T(8,128)S(1)} async-done(((f32[16,16,256]{2,1,0:T(8,128)}), f32[16,16,256]{2,1,0:T(8,128)S(1)}, u32[]{:S(2)}, u32[]{:S(2)}) %all-to-all-start.2) | async-done | bytes 262176 | tf_op jit(solution)/shard_map/all_to_all | solution.py:372
  72.9 0.7 copy-done.2
  73.6 3.4 %shard_map.119 = (f32[9,16,1024]{2,1,0:T(8,128)}, f32[10,16,1024]{2,1,0:T(8,128)}, f32[5,1,1024]{2,1,0:T(1,128)}, f32[5,1,1024]{2,1,0:T(1,128)}, f32[16,1024]{1,0:T(8,128)}) custom-call(s32[8]{0:T(128)} %pad_add_fusion.target_ref, f32[9,16,1024]{2,1,0:T(8,128)} %get-tuple-element.44.still_ref.still_in, f32[10,16,1024]{2,1,0:T(8,128)} %get-tuple-element.48.shifted_in, ...), custom_call_target="tpu_custom_call" | custom-call | tf_op jit(solution)/shard_map/pallas_call | solution.py:242
  77.1 0.5 collective-permute-start.7
  77.6 0.9 collective-permute-done.6.low_ref
  78.5 0.2 collective-permute-done.7.high_ref
  78.7 0.4 copy-done.13
  79.1 0.2 copy-done.16
  79.3 2.6 %shard_map.120 = (f32[10,16,1024]{2,1,0:T(8,128)}, f32[16,16,256]{2,1,0:T(8,128)}) custom-call(s32[8]{0:T(128)} %pad_add_fusion.target_ref, f32[9,16,1024]{2,1,0:T(8,128)} %get-tuple-element.50.still_ref.still_in, f32[10,16,1024]{2,1,0:T(8,128)} %get-tuple-element.51.moving_ref, f32[5,1,1024]{2,1,0:T(1,128)} %copy-done.13, f32[5,1,1024]{2,1,0:T(1,128)} %copy-done.16), custom_call_target="tpu_custom_call" | custom-call | tf_op jit(solution)/shard_map/pallas_call | solution.py:242
  81.9 3.7 %all-to-all-start.3 = ((f32[16,16,256]{2,1,0:T(8,128)}), f32[16,16,256]{2,1,0:T(8,128)S(1)}, u32[]{:S(2)}, u32[]{:S(2)}) async-start(f32[16,16,256]{2,1,0:T(8,128)} %get-tuple-element.55), calls=%async_computation.3 | async-start | bytes 524288 | tf_op jit(solution)/shard_map/all_to_all | solution.py:372
  85.7 0.2 copy.68
  86.0 1.1 gather_fusion.2
  87.2 1.1 gather_fusion.3
  88.4 1.1 gather_fusion.4
  89.6 6.6 %all-to-all-done.3.message_ref = f32[16,16,256]{2,1,0:T(8,128)S(1)} async-done(((f32[16,16,256]{2,1,0:T(8,128)}), f32[16,16,256]{2,1,0:T(8,128)S(1)}, u32[]{:S(2)}, u32[]{:S(2)}) %all-to-all-start.3) | async-done | bytes 262176 | tf_op jit(solution)/shard_map/all_to_all | solution.py:372
  96.1 0.7 copy-done.1
  96.8 2.9 %shard_map.121 = (f32[19,16,1024]{2,1,0:T(8,128)}, f32[16,1024]{1,0:T(8,128)}) custom-call(s32[8]{0:T(128)} %pad_add_fusion.target_ref, f32[9,16,1024]{2,1,0:T(8,128)} %get-tuple-element.50.still_ref.still_in, f32[10,16,1024]{2,1,0:T(8,128)} %get-tuple-element.54.shifted_in, f32[16,16,256]{2,1,0:T(8,128)} %copy-done.1), custom_call_target="tpu_custom_call" | custom-call | tf_op jit(solution)/shard_map/pallas_call | solution.py:242
  99.8 0.9 copy.82
  100.6 1.1 gather_fusion.5
  101.8 0.1 copy.62
  102.0 0.1 copy.61
  102.2 0.8 gather_fusion
  103.2 0.7 pad_maximum_fusion
  103.9 3.5 %all-to-all-start.4 = ((bf16[16,8,513]{2,1,0:T(8,128)(2,1)}), bf16[16,8,513]{2,1,0:T(8,128)(2,1)S(1)}, u32[]{:S(2)}, u32[]{:S(2)}) async-start(bf16[16,8,513]{2,1,0:T(8,128)(2,1)} %pad_maximum_fusion), calls=%async_computation.4 | async-start | bytes 327680 | tf_op jit(solution)/shard_map/all_to_all | solution.py:405
  107.6 0.3 cosine_convert_fusion
  108.0 7.3 %all-to-all-done.4 = bf16[16,8,513]{2,1,0:T(8,128)(2,1)S(1)} async-done(((bf16[16,8,513]{2,1,0:T(8,128)(2,1)}), bf16[16,8,513]{2,1,0:T(8,128)(2,1)S(1)}, u32[]{:S(2)}, u32[]{:S(2)}) %all-to-all-start.4) | async-done | bytes 131360 | tf_op jit(solution)/shard_map/all_to_all | solution.py:405
  115.4 0.3 convolution_convert_fusion
  115.7 0.2 fusion
  116.0 1.9 %all_gather.3 = bf16[128,262]{1,0:T(8,128)(2,1)S(1)} all-gather(bf16[64,262]{1,0:T(8,128)(2,1)S(1)} %pad_maximum_fusion.2), channel_id=1, replica_groups=mesh['blk'=16,'obs'=2] {'obs'}, dimensions={0}, use_global_device_ids=true | all-gather | bytes 100608 | tf_op jit(solution)/shard_map/all_gather | solution.py:413
  117.8 0.7 convert_element_type.49.panel_ref
  118.5 16.3 %shard_map.122 = f32[512,128]{1,0:T(8,128)} custom-call(f32[128,262]{1,0:T(8,128)} %convert_element_type.49.panel_ref, f32[3,512]{1,0:T(4,128)} %listen_ref.1), custom_call_target="tpu_custom_call" | custom-call | tf_op jit(solution)/shard_map/pallas_call | solution.py:242
  134.8 13.9 %all_to_all.30 = f32[16,32,128]{2,1,0:T(8,128)S(1)} all-to-all(f32[16,32,128]{2,1,0:T(8,128)} %bitcast.52), channel_id=1, replica_groups=mesh['blk'=16,'obs'=2] {'blk'}, dimensions={0} | all-to-all | bytes 524288 | tf_op jit(solution)/shard_map/all_to_all | solution.py:421
  148.8 0.6 reduce_sum.38
  (75 shorter events, 2.0 us)
Async XLA Ops:
  0.6 3.3 %copy-start.21 = (s32[1,4]{1,0:T(1,128)S(1)}, s32[1,4]{1,0:T(1,128)}, u32[]{:S(2)}) copy-start(s32[1,4]{1,0:T(1,128)} %param.13) | copy-start | bytes 52
  0.6 3.3 %copy-start.20 = (s32[1,4]{1,0:T(1,128)S(1)}, s32[1,4]{1,0:T(1,128)}, u32[]{:S(2)}) copy-start(s32[1,4]{1,0:T(1,128)} %param.14) | copy-start | bytes 52
  0.7 16.1 %copy-start = (s32[128]{0:T(128)S(1)}, s32[128]{0:T(128)}, u32[]{:S(2)}) copy-start(s32[128]{0:T(128)} %param.18) | copy-start | bytes 1540
  3.4 1.8 %collective-permute-start = (f32[5,1,1024]{2,1,0:T(1,128)}, f32[5,1,1024]{2,1,0:T(1,128)S(1)}, u32[]{:S(2)}, u32[]{:S(2)}) collective-permute-start(f32[5,1,1024]{2,1,0:T(1,128)} %get-tuple-element.34), channel_id=1, source_target_pairs={{0,1},{1,0},{2,3},{3,2},{4,5},{5,4},{6,7},{7,6},{8,9},{9,8},{10,11... | collective-permute-start | bytes 61448 | tf_op jit(solution)/shard_map/ppermute | solution.py:365
  3.9 1.4 collective-permute-start.1
  5.2 0.6 copy-start.10
  5.3 0.6 copy-start.14
  8.5 18.4 %all-to-all-start = ((f32[16,16,256]{2,1,0:T(8,128)}), f32[16,16,256]{2,1,0:T(8,128)S(1)}, u32[]{:S(2)}, u32[]{:S(2)}) async-start(f32[16,16,256]{2,1,0:T(8,128)} %get-tuple-element.37), calls=%async_computation | async-start | bytes 524288 | tf_op jit(solution)/shard_map/all_to_all | solution.py:372
  26.9 0.7 copy-start.3
  31.0 1.4 collective-permute-start.2
  31.0 1.6 %collective-permute-start.3 = (f32[5,1,1024]{2,1,0:T(1,128)}, f32[5,1,1024]{2,1,0:T(1,128)S(1)}, u32[]{:S(2)}, u32[]{:S(2)}) collective-permute-start(f32[5,1,1024]{2,1,0:T(1,128)} %get-tuple-element.41), channel_id=1, source_target_pairs={{1,0},{0,1},{3,2},{2,3},{5,4},{4,5},{7,6},{6,7},{9,8},{8,9},{11,10... | collective-permute-start | bytes 61448 | tf_op jit(solution)/shard_map/ppermute | solution.py:366
  32.4 0.6 copy-start.9
  32.5 0.6 copy-start.12
  35.7 14.1 %all-to-all-start.1 = ((f32[16,16,256]{2,1,0:T(8,128)}), f32[16,16,256]{2,1,0:T(8,128)S(1)}, u32[]{:S(2)}, u32[]{:S(2)}) async-start(f32[16,16,256]{2,1,0:T(8,128)} %get-tuple-element.43), calls=%async_computation.1 | async-start | bytes 524288 | tf_op jit(solution)/shard_map/all_to_all | solution.py:372
  49.8 0.7 copy-start.4
  53.9 1.4 collective-permute-start.4
  53.9 1.6 %collective-permute-start.5 = (f32[5,1,1024]{2,1,0:T(1,128)}, f32[5,1,1024]{2,1,0:T(1,128)S(1)}, u32[]{:S(2)}, u32[]{:S(2)}) collective-permute-start(f32[5,1,1024]{2,1,0:T(1,128)} %get-tuple-element.47), channel_id=1, source_target_pairs={{1,0},{0,1},{3,2},{2,3},{5,4},{4,5},{7,6},{6,7},{9,8},{8,9},{11,10... | collective-permute-start | bytes 61448 | tf_op jit(solution)/shard_map/ppermute | solution.py:366
  55.3 0.6 copy-start.11
  55.5 0.6 copy-start.15
  58.7 19.0 %copy-start.19 = (s32[128]{0:T(128)S(1)}, s32[128]{0:T(128)}, u32[]{:S(2)}) copy-start(s32[128]{0:T(128)} %param.15) | copy-start | bytes 1540
  58.7 14.3 %all-to-all-start.2 = ((f32[16,16,256]{2,1,0:T(8,128)}), f32[16,16,256]{2,1,0:T(8,128)S(1)}, u32[]{:S(2)}, u32[]{:S(2)}) async-start(f32[16,16,256]{2,1,0:T(8,128)} %get-tuple-element.49), calls=%async_computation.2 | async-start | bytes 524288 | tf_op jit(solution)/shard_map/all_to_all | solution.py:372
  72.9 0.7 copy-start.2
  77.0 8.5 %copy-start.5 = (bf16[128,512]{1,0:T(8,128)(2,1)S(1)}, bf16[128,512]{1,0:T(8,128)(2,1)}, u32[]{:S(2)}) copy-start(bf16[128,512]{1,0:T(8,128)(2,1)} %param.16) | copy-start | bytes 393220
  77.0 9.0 %copy-start.6 = (f32[16,1024]{1,0:T(8,128)S(1)}, f32[16,1024]{1,0:T(8,128)}, u32[]{:S(2)}) copy-start(f32[16,1024]{1,0:T(8,128)} %get-tuple-element.57) | copy-start | bytes 196612
  77.0 1.5 collective-permute-start.6
  77.1 1.6 %collective-permute-start.7 = (f32[5,1,1024]{2,1,0:T(1,128)}, f32[5,1,1024]{2,1,0:T(1,128)S(1)}, u32[]{:S(2)}, u32[]{:S(2)}) collective-permute-start(f32[5,1,1024]{2,1,0:T(1,128)} %get-tuple-element.53), channel_id=1, source_target_pairs={{1,0},{0,1},{3,2},{2,3},{5,4},{4,5},{7,6},{6,7},{9,8},{8,9},{11,10... | collective-permute-start | bytes 61448 | tf_op jit(solution)/shard_map/ppermute | solution.py:366
  78.5 0.6 copy-start.13
  78.7 0.6 copy-start.16
  79.3 7.9 %copy-start.7 = (f32[16,1024]{1,0:T(8,128)S(1)}, f32[16,1024]{1,0:T(8,128)}, u32[]{:S(2)}) copy-start(f32[16,1024]{1,0:T(8,128)} %get-tuple-element.58) | copy-start | bytes 196612
  81.9 6.5 %copy-start.8 = (f32[16,1024]{1,0:T(8,128)S(1)}, f32[16,1024]{1,0:T(8,128)}, u32[]{:S(2)}) copy-start(f32[16,1024]{1,0:T(8,128)} %get-tuple-element.59) | copy-start | bytes 196612
  81.9 14.3 %all-to-all-start.3 = ((f32[16,16,256]{2,1,0:T(8,128)}), f32[16,16,256]{2,1,0:T(8,128)S(1)}, u32[]{:S(2)}, u32[]{:S(2)}) async-start(f32[16,16,256]{2,1,0:T(8,128)} %get-tuple-element.55), calls=%async_computation.3 | async-start | bytes 524288 | tf_op jit(solution)/shard_map/all_to_all | solution.py:372
  96.1 0.7 copy-start.1
  101.8 5.6 %copy-start.17 = (bf16[3,64]{1,0:T(4,128)(2,1)S(1)}, bf16[3,64]{1,0:T(4,128)(2,1)}, u32[]{:S(2)}) copy-start(bf16[3,64]{1,0:T(4,128)(2,1)} %param.19) | copy-start | bytes 1156
  102.0 5.5 %copy-start.18 = (bf16[3,64]{1,0:T(4,128)(2,1)S(1)}, bf16[3,64]{1,0:T(4,128)(2,1)}, u32[]{:S(2)}) copy-start(bf16[3,64]{1,0:T(4,128)(2,1)} %param.20) | copy-start | bytes 1156
  103.9 11.4 %all-to-all-start.4 = ((bf16[16,8,513]{2,1,0:T(8,128)(2,1)}), bf16[16,8,513]{2,1,0:T(8,128)(2,1)S(1)}, u32[]{:S(2)}, u32[]{:S(2)}) async-start(bf16[16,8,513]{2,1,0:T(8,128)(2,1)} %pad_maximum_fusion), calls=%async_computation.4 | async-start | bytes 327680 | tf_op jit(solution)/shard_map/all_to_all | solution.py:405

commit v2 on v1

--- a/solution.py
+++ b/solution.py
@@ -1,3 +1,4 @@
+import functools
 import math
 
 import jax
@@ -94,11 +95,12 @@
     return out, density
 
 
-def emit_collided(load, still_ref, moving_ref, up_ref, down_ref, density_ref):
+def collide_all(field_ref, still_ref, moving_ref, up_ref, down_ref):
     depth = still_ref.shape[1]
-    for tile in range(still_ref.shape[2] // LANES):
-        lanes = slice(tile * LANES, (tile + 1) * LANES)
-        out, density = collide_tile([load(number, lanes) for number in range(19)])
+
+    def one_tile(tile, carry):
+        lanes = pl.ds(pl.multiple_of(tile * LANES, LANES), LANES)
+        out = collide_tile([field_ref[number, :, lanes] for number in range(19)])[0]
         for place, number in enumerate(still):
             still_ref[place, :, lanes] = out[number]
         for place, number in enumerate(x_order):
@@ -107,15 +109,9 @@
             up_ref[place, :, lanes] = out[number][depth - 1 : depth]
         for place, number in enumerate(x_minus):
             down_ref[place, :, lanes] = out[number][0:1]
-        if density_ref is not None:
-            density_ref[:, lanes] = density
-
-
-def first_kernel(field_ref, still_ref, moving_ref, up_ref, down_ref):
-    emit_collided(
-        lambda number, lanes: field_ref[number, :, lanes],
-        still_ref, moving_ref, up_ref, down_ref, None,
-    )
+        return carry
+
+    lax.fori_loop(0, still_ref.shape[2] // LANES, one_tile, 0)
 
 
 def lane_of(shape):
@@ -127,7 +123,7 @@
     return value if amount == 0 else pltpu.roll(value, amount, 1)
 
 
-def pack_kernel(target_ref, still_ref, moving_ref, low_ref, high_ref, shifted_ref, message_ref):
+def pack_pieces(still_ref, moving_ref, low_ref, high_ref, shifted_ref, piece_ref):
     depth = still_ref.shape[1]
     count = still_ref.shape[2]
     for place in range(5):
@@ -152,8 +148,8 @@
         for j in range(4):
             moved = turned(load(chosen[j], lanes), j * BS - begin)
             packed = jnp.where(small // BS == j, moved, packed)
-        message_ref[target_ref[piece], :, 0:LANES] = packed
-        message_ref[target_ref[piece], :, LANES:FACE] = turned(load(chosen[4], lanes), -begin)
+        piece_ref[piece, :, 0:LANES] = packed
+        piece_ref[piece, :, LANES:FACE] = turned(load(chosen[4], lanes), -begin)
     for piece, (chosen, begin) in enumerate([(z_downward, 0), (z_upward, BS - 1)]):
         gathered = jnp.zeros((depth, count), jnp.float32)
         for j in range(5):
@@ -165,12 +161,12 @@
                 tile = half * 4 + u
                 moved = turned(gathered[:, tile * LANES : (tile + 1) * LANES], 8 * u)
                 packed = jnp.where(small % BS // 8 == u, moved, packed)
-            message_ref[target_ref[2 + piece], :, half * LANES : (half + 1) * LANES] = packed
+            piece_ref[2 + piece, :, half * LANES : (half + 1) * LANES] = packed
     for piece, (number, lanes) in enumerate([(16, first), (18, first), (17, last), (15, last)]):
-        message_ref[target_ref[4 + piece], :, 0:LANES] = load(number, lanes)
-
-
-def stream_into(target_ref, still_ref, shifted_ref, message_ref, out_ref):
+        piece_ref[4 + piece, :, 0:LANES] = load(number, lanes)
+
+
+def stream_into(still_ref, shifted_ref, message_ref, out_ref):
     depth = still_ref.shape[1]
     count = still_ref.shape[2]
     small = lane_of((depth, LANES))
@@ -179,7 +175,7 @@
     for piece in range(2):
         tiles = []
         for half in range(2):
-            packed = message_ref[target_ref[2 + piece], :, half * LANES : (half + 1) * LANES]
+            packed = message_ref[2 + piece, :, half * LANES : (half + 1) * LANES]
             tiles += [turned(packed, -8 * u) for u in range(4)]
         columns.append(jnp.concatenate(tiles, axis=1))
     corners = {15: (4, 0, 127), 17: (5, 31, 96), 18: (6, 96, 31), 16: (7, 127, 0)}
@@ -202,7 +198,7 @@
             )
             j = chosen.index(number)
             begin = j // 4 * LANES
-            row = message_ref[target_ref[piece], :, begin : begin + LANES]
+            row = message_ref[piece, :, begin : begin + LANES]
             row = turned(row, edge - j % 4 * BS + shift_z)
             keep = small // BS == edge // BS
             if shift_z != 0:
@@ -211,28 +207,114 @@
             fixed = jnp.where(keep, row, old)
             if number in corners:
                 slot, lane_to, lane_from = corners[number]
-                corner = turned(message_ref[target_ref[slot], :, 0:LANES], lane_to - lane_from)
+                corner = turned(message_ref[slot, :, 0:LANES], lane_to - lane_from)
                 fixed = jnp.where(small == lane_to, corner, fixed)
             out_ref[number, :, lanes] = fixed
 
 
-def middle_kernel(
-    target_ref, still_in, shifted_in, message_ref,
-    still_ref, moving_ref, up_ref, down_ref, density_ref, field_ref,
+def window_kernel(
+    blocks, ring, target_ref, start_ref, field_ref, density_ref,
+    still_ref, moving_ref, shifted_ref, up_ref, down_ref, low_ref, high_ref,
+    piece_ref, send_ref, got_ref, edge_send, edge_got, send_sem, got_sem,
 ):
-    stream_into(target_ref, still_in, shifted_in, message_ref, field_ref)
-    emit_collided(
-        lambda number, lanes: field_ref[number, :, lanes],
-        still_ref, moving_ref, up_ref, down_ref, density_ref,
-    )
-
-
-def last_kernel(target_ref, still_in, shifted_in, message_ref, field_ref, density_ref):
-    stream_into(target_ref, still_in, shifted_in, message_ref, field_ref)
-    total = field_ref[0]
-    for number in range(1, 19):
-        total = total + field_ref[number]
-    density_ref[...] = total
+    mesh_ids = pl.DeviceIdType.MESH
+    me = lax.axis_index("blk")
+    side = lax.axis_index("obs")
+    right = lax.rem(side + 1, ring)
+    left = lax.rem(side + ring - 1, ring)
+    barrier = pltpu.get_barrier_semaphore()
+
+    def greet(distance, carry):
+        peer = lax.rem(me + distance, blocks)
+        pl.semaphore_signal(barrier, inc=1, device_id=(peer, side), device_id_type=mesh_ids)
+        return carry
+
+    for beside in (left, right):
+        pl.semaphore_signal(barrier, inc=1, device_id=(me, beside), device_id_type=mesh_ids)
+    lax.fori_loop(1, blocks, greet, 0)
+    field_ref[...] = start_ref[...]
+    pl.semaphore_wait(barrier, blocks + 1)
+
+    def one_step(step, carry):
+        collide_all(field_ref, still_ref, moving_ref, up_ref, down_ref)
+        edges = [
+            pltpu.make_async_remote_copy(
+                src_ref=source,
+                dst_ref=into.at[step],
+                send_sem=edge_send.at[step, way],
+                recv_sem=edge_got.at[step, way],
+                device_id=(me, beside),
+                device_id_type=mesh_ids,
+            )
+            for way, (source, into, beside) in enumerate(
+                [(up_ref, low_ref, right), (down_ref, high_ref, left)]
+            )
+        ]
+        for edge in edges:
+            edge.start()
+        for edge in edges:
+            edge.wait()
+        pack_pieces(
+            still_ref, moving_ref, low_ref.at[step], high_ref.at[step], shifted_ref, piece_ref
+        )
+
+        def copy_to(distance):
+            return pltpu.make_async_remote_copy(
+                src_ref=send_ref.at[distance],
+                dst_ref=got_ref.at[step, me],
+                send_sem=send_sem.at[step, distance],
+                recv_sem=got_sem.at[step, distance],
+                device_id=(lax.rem(me + distance, blocks), side),
+                device_id_type=mesh_ids,
+            )
+
+        def fill(distance, inner):
+            peer = lax.rem(me + distance, blocks)
+            near = jnp.zeros((send_ref.shape[1], LANES), jnp.float32)
+            rest = near
+            for piece in range(8):
+                wanted = target_ref[piece] == peer
+                near = jnp.where(wanted, piece_ref[piece, :, 0:LANES], near)
+                if piece < 4:
+                    rest = jnp.where(wanted, piece_ref[piece, :, LANES:FACE], rest)
+            send_ref[distance, :, 0:LANES] = near
+            send_ref[distance, :, LANES:FACE] = rest
+            return inner
+
+        def begin(distance, inner):
+            copy_to(distance).start()
+            return inner
+
+        def finish(distance, inner):
+            copy_to(distance).wait()
+            return inner
+
+        lax.fori_loop(1, blocks, fill, 0)
+        lax.fori_loop(1, blocks, begin, 0)
+        lax.fori_loop(1, blocks, finish, 0)
+
+        def choose(distance, held):
+            peer = lax.rem(me + distance, blocks)
+            near = got_ref[step, peer, :, 0:LANES]
+            rest = got_ref[step, peer, :, LANES:FACE]
+            wanted = [target_ref[piece] == peer for piece in range(8)]
+            return tuple(
+                jnp.where(wanted[at % 8], near if at < 8 else rest, held[at]) for at in range(12)
+            )
+
+        blank = jnp.zeros((send_ref.shape[1], LANES), jnp.float32)
+        held = lax.fori_loop(1, blocks, choose, (blank,) * 12)
+        for at in range(12):
+            half = at // 8 * LANES
+            piece_ref[at % 8, :, half : half + LANES] = held[at]
+        stream_into(still_ref, shifted_ref, piece_ref, field_ref)
+        total = field_ref[0]
+        for number in range(1, 19):
+            total = total + field_ref[number]
+        density_ref[step] = total
+        return carry
+
+    lax.fori_loop(0, STEPS, one_step, 0)
 
 
 def call(kernel, outs, scalars, *arrays, scratch=()):
@@ -351,37 +433,28 @@
     lane_count = lattice_state.shape[2]
     targets = jnp.concatenate([block_faces[0], block_edges[0]])
     ring = lax.axis_size("obs")
-    forward = [(i, (i + 1) % ring) for i in range(ring)]
-    backward = [(target, source) for source, target in forward]
     still_shape = (len(still), slab_depth, lane_count)
     moving_shape = (len(x_order), slab_depth, lane_count)
     edge_shape = (5, 1, lane_count)
-    collided_shapes = [still_shape, moving_shape, edge_shape, edge_shape]
-    plane_shape = (slab_depth, lane_count)
-    field_shape = (19, slab_depth, lane_count)
-    still_part, moving_part, up, down = call(first_kernel, collided_shapes, (), lattice_state)
-    densities = []
-    for turn_index in range(STEPS):
-        low = lax.ppermute(up, "obs", forward)
-        high = lax.ppermute(down, "obs", backward)
-        shifted, outgoing = call(
-            pack_kernel,
-            [moving_shape, (blocks, slab_depth, FACE)],
-            (targets,), still_part, moving_part, low, high,
-        )
-        received = lax.all_to_all(outgoing, "blk", split_axis=0, concat_axis=0, tiled=True)
-        if turn_index + 1 < STEPS:
-            still_part, moving_part, up, down, density = call(
-                middle_kernel,
-                collided_shapes + [plane_shape],
-                (targets,), still_part, shifted, received,
-                scratch=[field_shape],
-            )
-        else:
-            lattice_state, density = call(
-                last_kernel, [field_shape, plane_shape], (targets,), still_part, shifted, received
-            )
-        densities.append(density)
+    vmem = pl.BlockSpec(memory_space=pltpu.VMEM)
+    scratch = [
+        still_shape, moving_shape, moving_shape, edge_shape, edge_shape,
+        (STEPS,) + edge_shape, (STEPS,) + edge_shape,
+        (8, slab_depth, FACE), (blocks, slab_depth, FACE), (STEPS, blocks, slab_depth, FACE),
+    ]
+    lattice_state, densities = pl.pallas_call(
+        functools.partial(window_kernel, blocks, ring),
+        out_shape=[
+            jax.ShapeDtypeStruct((19, slab_depth, lane_count), jnp.float32),
+            jax.ShapeDtypeStruct((STEPS, slab_depth, lane_count), jnp.float32),
+        ],
+        in_specs=[pl.BlockSpec(memory_space=pltpu.SMEM), vmem],
+        out_specs=[vmem, vmem],
+        scratch_shapes=[pltpu.VMEM(shape, jnp.float32) for shape in scratch]
+        + [pltpu.SemaphoreType.DMA((STEPS, 2))] * 2
+        + [pltpu.SemaphoreType.DMA((STEPS, blocks))] * 2,
+        compiler_params=pltpu.CompilerParams(collective_id=0, has_side_effects=True),
+    )(targets, lattice_state)
     populations_out = lattice_state.reshape(1, 19, slab_depth, lane_count)
     readings = [jnp.take(density.reshape(-1), probe_cell) for density in densities]
     gained = pressure_gain * (jnp.stack(readings, axis=1) - 1.0)

time: 150 us -> 120 us (0.80)
  waiting for transfers between devices: 45.9 us -> 17.7 us
  Pallas kernels: 42.4 us -> 70.1 us
  starting transfers between devices: 24.7 us -> 9.4 us
  blocking collectives: 15.8 us -> 1.86 us
  local copies, waits for them, and re-layouts: 14.3 us -> 11.9 us
  other arithmetic: 4.08 us -> 6.1 us
    pallas_call x0 -> x1, Pallas kernels: none -> 53.8 us  [body(): pl.pallas_call(functools.partial(window_kernel, blocks, ring), out_shape=...]
    all_to_all x5 -> x1, waiting for transfers between devices: 42.9 us -> 7.32 us  [body(): lax.all_to_all(outgoing, 'blk', split_axis=0, concat_axis=0, tiled=True)]
    pallas_call x10 -> x1, Pallas kernels: 42.4 us -> 16.3 us  [call(): pl.pallas_call(kernel, out_shape=shapes, in_specs=[smem] * len(scalars) +...]
    all_to_all x5 -> x1, starting transfers between devices: 22.6 us -> 5.87 us  [body(): lax.all_to_all(outgoing, 'blk', split_axis=0, concat_axis=0, tiled=True)]
    all_to_all x1 -> x0, blocking collectives: 13.9 us -> none  [body(): lax.all_to_all(partial_value.reshape(blocks, listeners // blocks, 2 * BIN...]
    all_to_all x0 -> x1, waiting for transfers between devices: none -> 10.4 us  [body(): lax.all_to_all(partial_value.reshape(blocks, listeners // blocks, 2 * BIN...]
    unnamed x51 -> x19, local copies, waits for them, and re-layouts: 6.47 us -> 2.37 us
    all_to_all x0 -> x1, starting transfers between devices: none -> 3.53 us  [body(): lax.all_to_all(partial_value.reshape(blocks, listeners // blocks, 2 * BIN...]
  transfers between devices with their start and end apart: 13 -> 2, of which waited for: 12 -> 2; matrix products, arithmetic and copies ran while one was open for 5% -> 0% of each run, Pallas kernels for 0% -> 0%
where the time goes in v2:
time: 120 us; the launch traced here: 119 us
  Pallas kernels  70.1 us (58%)
  waiting for transfers between devices  17.7 us (15%)
  local copies, waits for them, and re-layouts  11.9 us (10%)
  starting transfers between devices  9.4 us (8%)
  other arithmetic  6.1 us (5%)
  blocking collectives  1.86 us (2%)
  between operations  1.59 us (1%)
    pallas_call x1, Pallas kernels, body(): pl.pallas_call(functools.partial(window_kernel, blocks, ring), out_shape=...  53.8 us
    pallas_call x1, Pallas kernels, call(): pl.pallas_call(kernel, out_shape=shapes, in_specs=[smem] * len(scalars) +...  16.3 us
    all_to_all x1, waiting for transfers between devices, body(): lax.all_to_all(partial_value.reshape(blocks, listeners // blocks, 2 * BIN...  10.4 us
    all_to_all x1, waiting for transfers between devices, body(): lax.all_to_all(outgoing, 'blk', split_axis=0, concat_axis=0, tiled=True)  7.32 us
    all_to_all x1, starting transfers between devices, body(): lax.all_to_all(outgoing, 'blk', split_axis=0, concat_axis=0, tiled=True)  5.87 us
    gather x4, local copies, waits for them, and re-layouts, body(): jnp.take(density.reshape(-1), probe_cell)  4.59 us
    all_to_all x1, starting transfers between devices, body(): lax.all_to_all(partial_value.reshape(blocks, listeners // blocks, 2 * BIN...  3.53 us
  transfers between devices with their start and end apart: 2, of which 2 were waited for; matrix products, arithmetic and copies ran while one was open for 0% of the time, Pallas kernels for 0%

profile of v2, /device:TPU:0, one launch (start us, length us, event | category | flops | bytes accessed | tf_op | source)
XLA Modules:
  0.0 119.1 jit_solution(8234267115565355697)
XLA Ops:
  0.6 0.8 slice.20
  1.5 0.0 copy-start.4
  1.5 1.0 fusion.25
  3.2 0.7 and_select_fusion
  3.8 0.1 fusion.14
  3.9 0.2 reduce_window_sum.11
  4.1 0.2 select_reduce_fusion.1
  4.3 0.7 add_select_fusion.2
  5.0 0.1 select_reduce_fusion
  5.1 0.1 reduce_sum.35
  5.1 0.1 reduce_sum.37
  5.2 0.1 fusion.11
  5.3 1.3 %pad_add_fusion.target_ref = s32[8]{0:T(128)} fusion(s32[4]{0:T(128)} %bitcast.66, s32[4]{0:T(128)} %bitcast.67), kind=kLoop, calls=%fused_computation.68 | loop fusion | flops 8 | bytes 64 | tf_op jit(solution)/shard_map/concatenate | solution.py:434
  6.6 53.8 %shard_map.113 = (f32[19,16,1024]{2,1,0:T(8,128)}, f32[4,16,1024]{2,1,0:T(8,128)}) custom-call(s32[8]{0:T(128)} %pad_add_fusion.target_ref, f32[19,16,1024]{2,1,0:T(8,128)} %bitcast.55), custom_call_target="tpu_custom_call" | custom-call | tf_op jit(solution)/shard_map/pallas_call | solution.py:445
  60.4 1.0 slice_bitcast_fusion.2
  61.4 0.0 copy-done.4
  61.4 0.0 copy-start
  61.4 1.1 gather_fusion.2
  62.6 1.1 gather_fusion.3
  63.8 1.1 gather_fusion.4
  65.0 1.1 gather_fusion.5
  66.1 0.1 copy.76
  66.3 0.1 copy.62
  66.4 0.1 copy.61
  66.6 0.0 copy-done
  66.6 1.2 %gather_fusion.1 = s32[128]{0:T(128)S(1)} fusion(s32[128]{0:T(128)S(1)} %copy-done, s32[1024]{0:T(1024)S(1)} %pad_clamp_fusion), kind=kCustom, calls=%fused_computation.5 | custom fusion | bytes 1536 | tf_op jit(solution)/shard_map/jit(_take)/gather | solution.py:404
  67.8 0.0 copy-start.2
  67.8 0.0 copy-start.3
  67.8 0.1 pad_maximum_fusion.1
  67.9 0.8 gather_fusion
  68.8 0.1 gather.18
  68.9 0.1 copy.66
  68.9 0.1 copy.63
  69.0 0.1 reduce_or.12
  69.1 0.1 copy.67
  69.2 0.1 copy.68
  69.4 0.1 bitcast_select_fusion
  69.5 0.7 pad_maximum_fusion
  70.2 5.9 %all-to-all-start = ((bf16[16,8,513]{2,1,0:T(8,128)(2,1)}), bf16[16,8,513]{2,1,0:T(8,128)(2,1)S(1)}, u32[]{:S(2)}, u32[]{:S(2)}) async-start(bf16[16,8,513]{2,1,0:T(8,128)(2,1)} %pad_maximum_fusion), calls=%async_computation | async-start | bytes 327680 | tf_op jit(solution)/shard_map/all_to_all | solution.py:478
  76.0 0.0 copy-start.1
  76.1 0.0 copy-done.2
  76.1 0.1 copy.72
  76.2 0.0 copy-done.3
  76.2 0.1 copy.73
  76.3 0.3 cosine_convert_fusion
  76.6 7.3 %all-to-all-done = bf16[16,8,513]{2,1,0:T(8,128)(2,1)S(1)} async-done(((bf16[16,8,513]{2,1,0:T(8,128)(2,1)}), bf16[16,8,513]{2,1,0:T(8,128)(2,1)S(1)}, u32[]{:S(2)}, u32[]{:S(2)}) %all-to-all-start) | async-done | bytes 131360 | tf_op jit(solution)/shard_map/all_to_all | solution.py:478
  84.0 0.1 convert_reduce_fusion
  84.1 0.3 convolution_convert_fusion
  84.4 0.2 fusion
  84.5 0.1 pad_maximum_fusion.2
  84.6 1.9 %all_gather.3 = bf16[128,262]{1,0:T(8,128)(2,1)S(1)} all-gather(bf16[64,262]{1,0:T(8,128)(2,1)S(1)} %pad_maximum_fusion.2), channel_id=1, replica_groups=mesh['blk'=16,'obs'=2] {'obs'}, dimensions={0}, use_global_device_ids=true | all-gather | bytes 100608 | tf_op jit(solution)/shard_map/all_gather | solution.py:486
  86.5 0.7 convert_element_type.49.panel_ref
  87.2 16.3 %shard_map.114 = f32[512,128]{1,0:T(8,128)} custom-call(f32[128,262]{1,0:T(8,128)} %convert_element_type.49.panel_ref, f32[3,512]{1,0:T(4,128)} %listen_ref.1), custom_call_target="tpu_custom_call" | custom-call | tf_op jit(solution)/shard_map/pallas_call | solution.py:324
  103.5 3.5 %all-to-all-start.1 = ((f32[16,32,128]{2,1,0:T(8,128)}), f32[16,32,128]{2,1,0:T(8,128)S(1)}, u32[]{:S(2)}, u32[]{:S(2)}) async-start(f32[16,32,128]{2,1,0:T(8,128)} %bitcast.57), calls=%async_computation.1 | async-start | bytes 524288 | tf_op jit(solution)/shard_map/all_to_all | solution.py:494
  107.1 10.4 %all-to-all-done.1 = f32[16,32,128]{2,1,0:T(8,128)S(1)} async-done(((f32[16,32,128]{2,1,0:T(8,128)}), f32[16,32,128]{2,1,0:T(8,128)S(1)}, u32[]{:S(2)}, u32[]{:S(2)}) %all-to-all-start.1) | async-done | bytes 262176 | tf_op jit(solution)/shard_map/all_to_all | solution.py:494
  117.5 0.6 reduce_sum.38
  118.1 0.0 copy-done.1
  118.1 1.0 copy.91
  (18 shorter events, 0.2 us)
Async XLA Ops:
  1.5 59.9 %copy-start.4 = (s32[128]{0:T(128)S(1)}, s32[128]{0:T(128)}, u32[]{:S(2)}) copy-start(s32[128]{0:T(128)} %param.15) | copy-start | bytes 1540
  61.4 5.1 %copy-start = (s32[128]{0:T(128)S(1)}, s32[128]{0:T(128)}, u32[]{:S(2)}) copy-start(s32[128]{0:T(128)} %param.18) | copy-start | bytes 1540
  67.8 8.3 %copy-start.2 = (bf16[3,64]{1,0:T(4,128)(2,1)S(1)}, bf16[3,64]{1,0:T(4,128)(2,1)}, u32[]{:S(2)}) copy-start(bf16[3,64]{1,0:T(4,128)(2,1)} %param.19) | copy-start | bytes 1156
  67.8 8.4 %copy-start.3 = (bf16[3,64]{1,0:T(4,128)(2,1)S(1)}, bf16[3,64]{1,0:T(4,128)(2,1)}, u32[]{:S(2)}) copy-start(bf16[3,64]{1,0:T(4,128)(2,1)} %param.20) | copy-start | bytes 1156
  70.2 13.8 %all-to-all-start = ((bf16[16,8,513]{2,1,0:T(8,128)(2,1)}), bf16[16,8,513]{2,1,0:T(8,128)(2,1)S(1)}, u32[]{:S(2)}, u32[]{:S(2)}) async-start(bf16[16,8,513]{2,1,0:T(8,128)(2,1)} %pad_maximum_fusion), calls=%async_computation | async-start | bytes 327680 | tf_op jit(solution)/shard_map/all_to_all | solution.py:478
  76.0 42.1 %copy-start.1 = (f32[19,16,1024]{2,1,0:T(8,128)S(1)}, f32[19,16,1024]{2,1,0:T(8,128)}, u32[]{:S(2)}) copy-start(f32[19,16,1024]{2,1,0:T(8,128)} %get-tuple-element.5) | copy-start | bytes 3735556
  103.5 14.0 %all-to-all-start.1 = ((f32[16,32,128]{2,1,0:T(8,128)}), f32[16,32,128]{2,1,0:T(8,128)S(1)}, u32[]{:S(2)}, u32[]{:S(2)}) async-start(f32[16,32,128]{2,1,0:T(8,128)} %bitcast.57), calls=%async_computation.1 | async-start | bytes 524288 | tf_op jit(solution)/shard_map/all_to_all | solution.py:494

commit v3 on v2

--- a/solution.py
+++ b/solution.py
@@ -338,7 +338,63 @@
     return jnp.concatenate([jnp.cos(phases), -jnp.sin(phases)], axis=1).astype(jnp.bfloat16)
 
 
-def radiate_kernel(panel_ref, listen_ref, out_ref, real_ref, imag_ref):
+def greet_peers(blocks):
+    me = lax.axis_index("blk")
+    side = lax.axis_index("obs")
+    barrier = pltpu.get_barrier_semaphore()
+
+    def greet(distance, carry):
+        pl.semaphore_signal(
+            barrier, inc=1, device_id=(lax.rem(me + distance, blocks), side),
+            device_id_type=pl.DeviceIdType.MESH,
+        )
+        return carry
+
+    lax.fori_loop(1, blocks, greet, 0)
+    return barrier
+
+
+def swap_pieces(blocks, send_ref, got_ref, send_sem, got_sem):
+    me = lax.axis_index("blk")
+    side = lax.axis_index("obs")
+
+    def copy_to(distance):
+        peer = lax.rem(me + distance, blocks)
+        return pltpu.make_async_remote_copy(
+            src_ref=send_ref.at[peer],
+            dst_ref=got_ref.at[me],
+            send_sem=send_sem.at[distance],
+            recv_sem=got_sem.at[distance],
+            device_id=(peer, side),
+            device_id_type=pl.DeviceIdType.MESH,
+        )
+
+    def begin(distance, inner):
+        copy_to(distance).start()
+        return inner
+
+    def finish(distance, inner):
+        copy_to(distance).wait()
+        return inner
+
+    lax.fori_loop(1, blocks, begin, 0)
+    lax.fori_loop(1, blocks, finish, 0)
+
+
+def exchange_kernel(blocks, source_ref, out_ref, got_ref, send_sem, got_sem):
+    me = lax.axis_index("blk")
+    barrier = greet_peers(blocks)
+    got_ref[me] = source_ref[me]
+    pl.semaphore_wait(barrier, blocks - 1)
+    swap_pieces(blocks, source_ref, got_ref, send_sem, got_sem)
+    out_ref[...] = got_ref[...]
+
+
+def radiate_kernel(
+    blocks, panel_ref, listen_ref, out_ref,
+    real_ref, imag_ref, full_ref, send_ref, got_ref, send_sem, got_sem,
+):
+    barrier = greet_peers(blocks)
     listeners = listen_ref.shape[1]
     real_ref[...] = jnp.zeros_like(real_ref)
     imag_ref[...] = jnp.zeros_like(imag_ref)
@@ -382,7 +438,15 @@
 
     lax.fori_loop(0, panel_ref.shape[0] // 8, accumulate, 0)
     both = jnp.concatenate([jnp.sum(real_ref[...], axis=1), jnp.sum(imag_ref[...], axis=1)], axis=0)
-    out_ref[...] = both.T
+    full_ref[...] = both.T
+    chunk = out_ref.shape[0]
+    for number in range(blocks):
+        send_ref[number] = full_ref[number * chunk : (number + 1) * chunk]
+    me = lax.axis_index("blk")
+    got_ref[me] = send_ref[me]
+    pl.semaphore_wait(barrier, blocks - 1)
+    swap_pieces(blocks, send_ref, got_ref, send_sem, got_sem)
+    out_ref[...] = jnp.sum(got_ref[...], axis=0)
 
 
 def route_slots(payload, owners, alive_slot, blocks):
@@ -475,7 +539,15 @@
     count_slots = recent.shape[0]
     alive_slot = jnp.arange(count_slots, dtype=jnp.int32) < panel_count[0]
     outgoing = route_slots(recent, panel_owner, alive_slot, blocks)
-    incoming = lax.all_to_all(outgoing, "blk", split_axis=0, concat_axis=0, tiled=True)
+    incoming = pl.pallas_call(
+        functools.partial(exchange_kernel, blocks),
+        out_shape=jax.ShapeDtypeStruct(outgoing.shape, outgoing.dtype),
+        in_specs=[vmem],
+        out_specs=vmem,
+        scratch_shapes=[pltpu.VMEM(outgoing.shape, outgoing.dtype)]
+        + [pltpu.SemaphoreType.DMA((blocks,))] * 2,
+        compiler_params=pltpu.CompilerParams(collective_id=1, has_side_effects=True),
+    )(outgoing)
     owned = settle(incoming).reshape(P_OWN, 2, SAMPLES)
     spectra = (
         jnp.einsum("pgt,tk->pgk", owned, transform, preferred_element_type=jnp.float32)
@@ -485,17 +557,23 @@
     panels = jnp.concatenate([spectra, panel_pos.T, panel_normal.T], axis=1)
     gathered = lax.all_gather(panels, "obs", axis=0, tiled=True).astype(jnp.float32)
     listeners = observers.shape[1]
-    partial_value = call(
-        radiate_kernel,
-        [(listeners, 2 * BINS)],
-        (), gathered, observers,
-        scratch=[(BINS, 8, listeners), (BINS, 8, listeners)],
-    )[0]
-    pieces = lax.all_to_all(
-        partial_value.reshape(blocks, listeners // blocks, 2 * BINS),
-        "blk", split_axis=0, concat_axis=0, tiled=True,
-    )
-    return (populations_out, jnp.sum(pieces, axis=0)[None])
+    chunk = listeners // blocks
+    spectrum = pl.pallas_call(
+        functools.partial(radiate_kernel, blocks),
+        out_shape=jax.ShapeDtypeStruct((chunk, 2 * BINS), jnp.float32),
+        in_specs=[vmem, vmem],
+        out_specs=vmem,
+        scratch_shapes=[
+            pltpu.VMEM(shape, jnp.float32)
+            for shape in [
+                (BINS, 8, listeners), (BINS, 8, listeners), (listeners, 2 * BINS),
+                (blocks, chunk, 2 * BINS), (blocks, chunk, 2 * BINS),
+            ]
+        ]
+        + [pltpu.SemaphoreType.DMA((blocks,))] * 2,
+        compiler_params=pltpu.CompilerParams(collective_id=2, has_side_effects=True),
+    )(gathered, observers)
+    return (populations_out, spectrum[None])
 
 
 def solution(mesh):

time: 120 us -> 109 us (0.908)
  waiting for transfers between devices: 17.7 us -> 0 us
  Pallas kernels: 70.1 us -> 87.7 us
  starting transfers between devices: 9.4 us -> 0 us
  other arithmetic: 6.1 us -> 4.12 us
    all_to_all x2 -> x0, waiting for transfers between devices: 17.7 us -> none  [the longest x1 10.4 us: body(): lax.all_to_all(partial_value.reshape(blocks, listeners // blocks, 2 * BIN...]
    pallas_call x1 -> x2, Pallas kernels: 16.3 us -> 33.9 us  [the longest x1 23.3 us: body(): pl.pallas_call(functools.partial(radiate_kernel, blocks), out_shape=jax.S...]
    all_to_all x2 -> x0, starting transfers between devices: 9.4 us -> none  [the longest x1 5.87 us: body(): lax.all_to_all(outgoing, 'blk', split_axis=0, concat_axis=0, tiled=True)]
    unnamed x19 -> x25, local copies, waits for them, and re-layouts: 2.37 us -> 3.07 us
  transfers between devices with their start and end apart: 2 -> 0, of which waited for: 2 -> 0; matrix products, arithmetic and copies ran while one was open for 0% -> 0% of each run, Pallas kernels for 0% -> 0%
where the time goes in v3:
time: 109 us; the launch traced here: 108 us
  Pallas kernels  87.7 us (80%)
  local copies, waits for them, and re-layouts  11.7 us (11%)
  other arithmetic  4.12 us (4%)
  blocking collectives  1.87 us (2%)
  between operations  1.64 us (2%)
  matrix products  1.35 us (1%)
    pallas_call x1, Pallas kernels, body(): pl.pallas_call(functools.partial(window_kernel, blocks, ring), out_shape=...  53.8 us
    pallas_call x1, Pallas kernels, body(): pl.pallas_call(functools.partial(radiate_kernel, blocks), out_shape=jax.S...  23.3 us
    pallas_call x1, Pallas kernels, body(): pl.pallas_call(functools.partial(exchange_kernel, blocks), out_shape=jax....  10.7 us
    gather x4, local copies, waits for them, and re-layouts, body(): jnp.take(density.reshape(-1), probe_cell)  4.59 us
    unnamed x25, local copies, waits for them, and re-layouts  3.07 us

profile of v3, /device:TPU:0, one launch (start us, length us, event | category | flops | bytes accessed | tf_op | source)
XLA Modules:
  0.0 108.3 jit_solution(14546182929525627522)
XLA Ops:
  0.6 0.0 copy-start.6
  0.6 1.3 %pad_add_fusion.target_ref = s32[8]{0:T(128)} fusion(s32[4]{0:T(128)} %bitcast.67, s32[4]{0:T(128)} %bitcast.68), kind=kLoop, calls=%fused_computation.67 | loop fusion | flops 8 | bytes 64 | tf_op jit(solution)/shard_map/concatenate | solution.py:498
  1.9 53.8 %shard_map.113 = (f32[19,16,1024]{2,1,0:T(8,128)}, f32[4,16,1024]{2,1,0:T(8,128)}) custom-call(s32[8]{0:T(128)} %pad_add_fusion.target_ref, f32[19,16,1024]{2,1,0:T(8,128)} %bitcast.57), custom_call_target="tpu_custom_call" | custom-call | tf_op jit(solution)/shard_map/pallas_call | solution.py:509
  55.7 1.0 slice_bitcast_fusion.2
  56.7 0.0 copy-done.6
  56.7 0.0 copy-start.2
  56.7 1.1 %gather_fusion.2 = f32[128]{0:T(128)S(1)} fusion(f32[16384]{0:T(1024)S(1)} %bitcast.53, s32[1024]{0:T(1024)S(1)} %pad_clamp_fusion.1), kind=kCustom, calls=%fused_computation.clone | custom fusion | bytes 1536 | tf_op jit(solution)/shard_map/jit(_take)/gather | solution.py:523
  57.9 0.0 copy-start
  57.9 1.1 %gather_fusion.3 = f32[128]{0:T(128)S(1)} fusion(f32[16384]{0:T(1024)S(1)} %bitcast.55, s32[1024]{0:T(1024)S(1)} %pad_clamp_fusion.1), kind=kCustom, calls=%fused_computation.1.clone | custom fusion | bytes 1536 | tf_op jit(solution)/shard_map/jit(_take)/gather | solution.py:523
  59.1 1.1 %gather_fusion.4 = f32[128]{0:T(128)S(1)} fusion(f32[16384]{0:T(1024)S(1)} %bitcast.56, s32[1024]{0:T(1024)S(1)} %pad_clamp_fusion.1), kind=kCustom, calls=%fused_computation.2.clone | custom fusion | bytes 1536 | tf_op jit(solution)/shard_map/jit(_take)/gather | solution.py:523
  60.3 1.1 %gather_fusion.5 = f32[128]{0:T(128)S(1)} fusion(f32[16384]{0:T(1024)S(1)} %bitcast.54, s32[1024]{0:T(1024)S(1)} %pad_clamp_fusion.1), kind=kCustom, calls=%fused_computation.3.clone | custom fusion | bytes 1536 | tf_op jit(solution)/shard_map/jit(_take)/gather | solution.py:523
  61.5 0.0 copy-done.2
  61.5 0.1 slice.20
  61.5 0.1 copy.86
  61.7 0.1 copy.72
  61.8 0.1 copy.71
  61.9 0.1 fusion.25
  62.1 0.1 pad_maximum_fusion.1
  62.8 0.0 copy-done
  62.8 0.1 fusion.17
  63.0 0.2 reduce_window_sum.11
  63.1 0.2 select_reduce_fusion.1
  63.3 0.1 select_reduce_fusion
  63.5 0.8 gather_fusion
  64.3 0.0 copy-start.4
  64.3 0.0 copy-start.5
  64.3 0.1 reduce_sum.26
  64.4 0.1 bitcast_select_fusion
  64.5 1.2 %gather_fusion.1 = s32[128]{0:T(128)S(1)} fusion(s32[128]{0:T(128)S(1)} %copy-done, s32[1024]{0:T(1024)S(1)} %pad_clamp_fusion), kind=kCustom, calls=%fused_computation.5 | custom fusion | bytes 1536 | tf_op jit(solution)/shard_map/jit(_take)/gather | solution.py:468
  65.8 0.0 copy-start.1
  65.8 0.2 gather.38
  66.0 0.2 reduce_sum.29
  66.2 0.1 fusion.14
  66.3 0.2 reduce_or.13
  66.5 0.1 fusion.4
  66.6 0.7 pad_maximum_fusion.source_ref
  67.3 10.7 %shard_map.114 = bf16[16,8,513]{2,1,0:T(8,128)(2,1)} custom-call(bf16[16,8,513]{2,1,0:T(8,128)(2,1)} %pad_maximum_fusion.source_ref), custom_call_target="tpu_custom_call" | custom-call | tf_op jit(solution)/shard_map/pallas_call | solution.py:542
  77.9 0.8 slice.36
  78.7 0.1 copy.87
  78.8 1.2 %convolution_convert_fusion = bf16[64,512]{1,0:T(8,128)(2,1)S(1)} fusion(bf16[128,513]{1,0:T(8,128)(2,1)} %bitcast.60, s32[128]{0:T(128)S(1)} %bitcast_convert_fusion), kind=kOutput, calls=%fused_computation.6 | convolution fusion | flops 8429568 | bytes 197120 | tf_op jit(solution)/shard_map/rp,rw->pw/dot_general | solution.py:477
  80.0 0.3 cosine_convert_fusion
  80.3 0.2 fusion
  80.5 0.0 copy-done.4
  80.5 0.1 copy.82
  80.7 0.0 copy-done.5
  80.7 0.1 copy.83
  80.8 0.1 pad_maximum_fusion.2
  80.9 1.9 %all_gather.3 = bf16[128,262]{1,0:T(8,128)(2,1)S(1)} all-gather(bf16[64,262]{1,0:T(8,128)(2,1)S(1)} %pad_maximum_fusion.2), channel_id=1, replica_groups=mesh['blk'=16,'obs'=2] {'obs'}, dimensions={0}, use_global_device_ids=true | all-gather | bytes 100608 | tf_op jit(solution)/shard_map/all_gather | solution.py:558
  82.7 0.7 convert_element_type.49.panel_ref
  83.4 23.3 %shard_map.115 = f32[32,128]{1,0:T(8,128)} custom-call(f32[128,262]{1,0:T(8,128)} %convert_element_type.49.panel_ref, f32[3,512]{1,0:T(4,128)} %listen_ref.1), custom_call_target="tpu_custom_call" | custom-call | tf_op jit(solution)/shard_map/pallas_call | solution.py:561
  106.7 0.0 copy-done.1
  106.7 0.0 copy-start.3
  106.7 1.0 copy.103
  107.7 0.0 copy-done.3
  107.7 0.6 copy.104
  (20 shorter events, 0.2 us)
Async XLA Ops:
  0.6 56.0 %copy-start.6 = (s32[128]{0:T(128)S(1)}, s32[128]{0:T(128)}, u32[]{:S(2)}) copy-start(s32[128]{0:T(128)} %param.15) | copy-start | bytes 1540
  56.7 4.8 %copy-start.2 = (bf16[128,512]{1,0:T(8,128)(2,1)S(1)}, bf16[128,512]{1,0:T(8,128)(2,1)}, u32[]{:S(2)}) copy-start(bf16[128,512]{1,0:T(8,128)(2,1)} %param.16) | copy-start | bytes 393220
  57.9 4.9 %copy-start = (s32[128]{0:T(128)S(1)}, s32[128]{0:T(128)}, u32[]{:S(2)}) copy-start(s32[128]{0:T(128)} %param.18) | copy-start | bytes 1540
  64.3 16.2 %copy-start.4 = (bf16[3,64]{1,0:T(4,128)(2,1)S(1)}, bf16[3,64]{1,0:T(4,128)(2,1)}, u32[]{:S(2)}) copy-start(bf16[3,64]{1,0:T(4,128)(2,1)} %param.19) | copy-start | bytes 1156
  64.3 16.3 %copy-start.5 = (bf16[3,64]{1,0:T(4,128)(2,1)S(1)}, bf16[3,64]{1,0:T(4,128)(2,1)}, u32[]{:S(2)}) copy-start(bf16[3,64]{1,0:T(4,128)(2,1)} %param.20) | copy-start | bytes 1156
  65.8 40.9 %copy-start.1 = (f32[19,16,1024]{2,1,0:T(8,128)S(1)}, f32[19,16,1024]{2,1,0:T(8,128)}, u32[]{:S(2)}) copy-start(f32[19,16,1024]{2,1,0:T(8,128)} %get-tuple-element.5) | copy-start | bytes 3735556
  106.7 1.1 copy-start.3
